TPU v7x, 32 devices: a whole 2x2x4 slice. The times are simulated.
32 devices in a mesh: ens: 2 (over y), hist: 4 (over z), mom: 2 (over x), rep: 2 (over core).
Axes of the slice: x: 2, y: 2, z: 4, core: 2. Of those that a mesh axis runs over, the one named last changes fastest.
Arguments:
- history_stat: float32 [512, 1024, 512], P(('hist', 'rep'), 'ens', 'mom'), parts along dimension 1, may hold values from -6 to 6, as said below
- history_spec: float32 [512, 1024, 512], P(('hist', 'rep'), 'ens', 'mom'), parts along dimension 1, may hold values from -6 to 6, as said below
Outputs:
- rows_stat: float32 [6, 512, 512], P('ens', ('hist', 'rep'), 'mom'), parts along dimension 0
- rows_spec: float32 [6, 512, 512], P('ens', ('hist', 'rep'), 'mom'), parts along dimension 0
- newest_stat: float32 [10, 5, 512], P('ens', None, 'mom'), parts along dimension 0
- newest_spec: float32 [10, 5, 512], P('ens', None, 'mom'), parts along dimension 0
There are 2 independent parts, one for each index of `ens`. A program takes and returns all parts, laid end to end along the dimension named above; each array names one. Nothing has to cross between parts.
Inputs may be any that keep to these rules, and one draw needn't show every extreme that they name: `history_stat`: symmetric under exchange of its two time indices. `history_spec`: antisymmetric under exchange of its two time indices, zero where they are equal.
All inputs are finite; a program needn't handle non-finite values.
Results may differ from a plain program's by a relative error of at most 0.0003.
Values sent between devices are 32-bit elements; how exact they have to be, the bound alone decides.
No kernel may reach another device: no remote copies, remote signals or barrier semaphores. Data moves between devices by JAX's collectives and lax.ppermute only.
A program may use at most 128 MiB of HBM per device.

v0:
```python
import functools
import math

import jax
import jax.numpy as jnp
import numpy as np
from jax import lax
from jax.experimental import pallas as pl
from jax.experimental.pallas import tpu as pltpu
from jax.sharding import PartitionSpec as P

MOMENTA = 512
STEPS = 3
TIME_STEP = 0.12
CUTOFF = 12.8
MASS_SQUARED = 1.0
SUNSET_COUPLING = 100.0
HARTREE_COUPLING = 2.45
HIGHEST = lax.Precision.HIGHEST

SUB = 8
LANES = 128
WIDE = 32
RESIDENT_BYTES = 40 * 2**20
PART_ROWS = 16
EXTRA = 32
F32 = jnp.float32
VMEM = pl.BlockSpec(memory_space=pltpu.VMEM)
HBM = pl.BlockSpec(memory_space=pltpu.HBM)
SMEM = pl.BlockSpec(memory_space=pltpu.SMEM)


def params(mib):
    return pltpu.CompilerParams(vmem_limit_bytes=mib * 2**20)


def tables(points):
    index = np.arange(points, dtype=np.int64) + 1
    momentum_step = CUTOFF / points
    radius_step = math.pi / ((points + 1) * momentum_step)
    sine = np.sin((index[:, None] * index[None, :]) % (2 * (points + 1)) * (math.pi / (points + 1)))
    momentum = index * momentum_step
    radius = index * radius_step
    forward = sine * (momentum[:, None] * momentum_step) / (2.0 * math.pi**2 * radius[None, :])
    backward = sine * (4.0 * math.pi * radius_step * radius[:, None]) / momentum[None, :]
    measure = momentum * momentum * momentum_step / (2.0 * math.pi**2)
    return tuple(np.asarray(a, np.float32) for a in (forward, backward, measure, momentum))


def shifts(size, amount):
    return [(i, (i + amount) % size) for i in range(size)]


def first_kernel(stat_hbm, spec_hbm, c0, c1, d0, d1, out_ref, stat_ref, spec_ref, sem):
    rows, _, width = stat_ref.shape
    latest = pl.ds(stat_hbm.shape[1] - SUB, SUB)
    copies = [
        pltpu.make_async_copy(stat_hbm.at[:, latest], stat_ref, sem.at[0]),
        pltpu.make_async_copy(spec_hbm.at[:, latest], spec_ref, sem.at[1]),
    ]
    for c in copies:
        c.start()
    for c in copies:
        c.wait()
    c0[...] = stat_ref[:, SUB - 2, :]
    c1[...] = stat_ref[:, SUB - 1, :]
    d0[...] = -spec_ref[:, SUB - 2, :]
    d1[...] = -spec_ref[:, SUB - 1, :]
    half = rows + SUB
    out_ref[0:rows, :] = c1[...]
    out_ref[half : half + rows, :] = d1[...]
    out_ref[rows:half, :] = jnp.zeros((SUB, width), F32)
    out_ref[half + rows :, :] = jnp.zeros((SUB, width), F32)


def load_kernel(counts, *refs):
    n = len(counts)
    sources, outs, sem = refs[:n], refs[n + 1 : 2 * n + 1], refs[-1]
    copies = [
        pltpu.make_async_copy(sources[i].at[pl.ds(start, count)], outs[i], sem.at[i])
        for i, (start, count) in enumerate(counts)
    ]
    for c in copies:
        c.start()
    for c in copies:
        c.wait()


def load(sources, counts, order):
    return pl.pallas_call(
        functools.partial(load_kernel, counts),
        out_shape=[pltpu.VMEM((n,) + s.shape[1:], F32) for s, (_, n) in zip(sources, counts)],
        in_specs=[HBM] * len(sources) + [VMEM],
        out_specs=[VMEM] * len(sources),
        scratch_shapes=[pltpu.SemaphoreType.DMA((len(sources),))],
        compiler_params=params(2),
        name="load",
    )(*sources, order)


def transform_kernel(step, blocks, *refs):
    current = step + 1
    place = refs[0]
    pieces = refs[1 : 1 + blocks]
    forward, backward, measure = refs[1 + blocks : 4 + blocks]
    stats = refs[4 + blocks : 5 + blocks + current]
    specs = refs[5 + blocks + current : 6 + blocks + 2 * current]
    out_ref, own_ref = refs[6 + blocks + 2 * current :]
    rows, width = stats[0].shape
    half = rows + SUB
    own = place[0]
    times = place[1] * rows
    radial = None
    tadpole = None
    for k in range(blocks):
        block = lax.rem(own + (blocks - k), blocks)
        part = jnp.dot(pieces[k][...], forward[block], precision=HIGHEST, preferred_element_type=F32)
        radial = part if radial is None else radial + part
        line = rows - 1 if step == 0 else rows + current
        part = jnp.sum(pieces[k][line : line + 1, :] * measure[block], axis=1, keepdims=True)
        tadpole = part if tadpole is None else tadpole + part
    stat = radial[:half]
    spec = radial[half:]
    square_stat = stat * stat
    square_spec = spec * spec
    sigma_stat = -SUNSET_COUPLING * stat * (square_stat - 0.75 * square_spec)
    sigma_spec = -SUNSET_COUPLING * spec * (3.0 * square_stat - 0.25 * square_spec)
    sigma = jnp.concatenate([sigma_stat, sigma_spec], axis=0)
    sigma = jnp.dot(sigma, backward[own], precision=HIGHEST, preferred_element_type=F32)
    group_stat = sigma[:rows]
    group_spec = sigma[half : half + rows]
    out_ref[0:rows, :] = group_stat
    out_ref[rows : 2 * rows, :] = group_spec
    own_ref[0:SUB, :] = sigma[rows:half]
    own_ref[SUB : 2 * SUB, :] = sigma[half + rows :]
    row_times = times + lax.broadcasted_iota(jnp.int32, (rows, width), 0)
    index = lax.broadcasted_iota(jnp.int32, (SUB, width), 0)
    base = 2 * rows
    sums_stat = jnp.zeros((SUB, width), F32)
    sums_spec = jnp.zeros((SUB, width), F32)
    last = place[2]
    for a in range(current + 1):
        column_stat = stats[a][...]
        column_spec = specs[a][...]
        later = row_times <= last - 1 + a
        earlier = row_times >= last - 1 + a
        partial = -group_spec * column_stat - jnp.where(later, group_stat * column_spec, 0.0)
        sums_stat = jnp.where(index == a, jnp.sum(partial, axis=0, keepdims=True), sums_stat)
        partial = jnp.where(earlier, group_spec * column_spec, 0.0)
        sums_spec = jnp.where(index == a, jnp.sum(partial, axis=0, keepdims=True), sums_spec)
    out_ref[base : base + SUB, :] = sums_stat
    out_ref[base + SUB : base + 2 * SUB, :] = sums_spec
    out_ref[base + 2 * SUB : base + 3 * SUB, :] = jnp.concatenate(
        [r[rows - 2 : rows, :] for r in (stats[0], stats[1], specs[0], specs[1])], axis=0
    )
    out_ref[base + 3 * SUB :, :] = jnp.broadcast_to(tadpole, (SUB, width))


def memory_kernel(step, group_sizes, resident, stream, *refs):
    current = step + 1
    newest = STEPS + 2
    hists, reps = group_sizes
    groups = hists * reps
    refs = list(refs)

    def take(n):
        head = refs[:n]
        del refs[:n]
        return head

    (place,) = take(1)
    pieces = take(groups)
    (own_ref, momentum) = take(2)
    stats = take(current + 1)
    specs = take(current + 1)
    blocks_in = take(2) if step else None
    stat_parts = take(len(resident[0]))
    spec_parts = take(len(resident[1]))
    hbm = take(1) if stream else None
    last_step = step == STEPS - 1
    if last_step:
        rows_stat, rows_spec, block_stat, block_spec = take(4)
    else:
        next_stat_ref, next_spec_ref, block_stat, block_spec, out_ref = take(5)
    sig_stat, sig_spec, extra, mem_stat, mem_spec = take(5)
    if stream:
        buffers, sem = take(2)
    rows, width = stats[0].shape
    times = groups * rows
    hist, rep = place[3], place[4]
    group = hist * reps + rep
    chunks = rows // SUB

    def copy(c):
        slot = (c - stream[0]) % 2
        return pltpu.make_async_copy(hbm[0].at[pl.ds(c * SUB, SUB)], buffers.at[slot], sem.at[slot])

    if stream:
        for c in range(stream[0], min(stream[0] + 2, chunks)):
            copy(c).start()
    for k in range(hists):
        for q in range(reps):
            piece = pieces[k * reps + q]
            who = lax.rem(hist + (hists - k), hists) * reps + lax.rem(rep + (reps - q), reps)
            at = pl.multiple_of(who * rows, SUB)
            sig_stat[pl.ds(at, rows), :] = piece[0:rows, :]
            sig_spec[pl.ds(at, rows), :] = piece[rows : 2 * rows, :]
            extra[who] = piece[2 * rows :, :]

    def find(parts, sizes, c):
        start = c * SUB
        for ref, (first, count) in zip(parts, sizes):
            if first <= start < first + count:
                return ref, start - first
        return None, 0

    tile = lax.broadcasted_iota(jnp.int32, (SUB, LANES), 0)
    for c in range(chunks):
        stat_ref, stat_at = find(stat_parts, resident[0], c)
        spec_ref, spec_at = find(spec_parts, resident[1], c)
        if spec_ref is None:
            copy(c).wait()
            spec_ref, spec_at = buffers.at[(c - stream[0]) % 2], 0
        first_time = group * rows + c * SUB
        middle = first_time // WIDE
        for l in range(width // LANES):
            lane = slice(l * LANES, (l + 1) * LANES)

            def below(j, acc, stat_ref=stat_ref, stat_at=stat_at, spec_ref=spec_ref, spec_at=spec_at, lane=lane):
                acc_stat, acc_spec = list(acc[0]), list(acc[1])
                for t in range(WIDE // SUB):
                    at = pl.ds(pl.multiple_of(j * WIDE + t * SUB, SUB), SUB)
                    weight_stat, weight_spec = sig_stat[at, lane], sig_spec[at, lane]
                    for r in range(SUB):
                        acc_stat[r] += weight_spec * stat_ref[stat_at + r, at, lane]
                        acc_stat[r] += weight_stat * spec_ref[spec_at + r, at, lane]
                return tuple(acc_stat), tuple(acc_spec)

            def above(j, acc, stat_ref=stat_ref, stat_at=stat_at, spec_ref=spec_ref, spec_at=spec_at, lane=lane):
                acc_stat, acc_spec = list(acc[0]), list(acc[1])
                for t in range(WIDE // SUB):
                    at = pl.ds(pl.multiple_of(j * WIDE + t * SUB, SUB), SUB)
                    weight_spec = sig_spec[at, lane]
                    for r in range(SUB):
                        acc_stat[r] += weight_spec * stat_ref[stat_at + r, at, lane]
                        acc_spec[r] += weight_spec * spec_ref[spec_at + r, at, lane]
                return tuple(acc_stat), tuple(acc_spec)

            zero = jnp.zeros((SUB, LANES), F32)
            acc = (tuple(zero for _ in range(SUB)), tuple(zero for _ in range(SUB)))
            acc = lax.fori_loop(0, middle, below, acc)
            acc_stat, acc_spec = list(acc[0]), list(acc[1])
            for t in range(WIDE // SUB):
                start = pl.multiple_of(middle * WIDE + t * SUB, SUB)
                at = pl.ds(start, SUB)
                weight_stat, weight_spec = sig_stat[at, lane], sig_spec[at, lane]
                for r in range(SUB):
                    value = spec_ref[spec_at + r, at, lane]
                    early = start + tile <= first_time + r
                    acc_stat[r] += weight_spec * stat_ref[stat_at + r, at, lane]
                    acc_stat[r] += jnp.where(early, weight_stat * value, 0.0)
                    acc_spec[r] += jnp.where(early, 0.0, weight_spec * value)
            acc = (tuple(acc_stat), tuple(acc_spec))
            acc = lax.fori_loop(middle + 1, times // WIDE, above, acc)
            mem_stat[c * SUB : (c + 1) * SUB, lane] = -jnp.concatenate(
                [jnp.sum(a, axis=0, keepdims=True) for a in acc[0]], axis=0
            )
            mem_spec[c * SUB : (c + 1) * SUB, lane] = jnp.concatenate(
                [jnp.sum(a, axis=0, keepdims=True) for a in acc[1]], axis=0
            )
        if stream and c >= stream[0] and c + 2 < chunks:
            copy(c + 2).start()

    factor = TIME_STEP * TIME_STEP
    corner = extra[groups - 1]
    index = lax.broadcasted_iota(jnp.int32, (SUB, width), 0)
    zero = jnp.zeros((SUB, width), F32)
    if step == 0:
        def pick(first, sign):
            out = []
            for a in range(2):
                left = corner[2 * SUB + first + a : 2 * SUB + first + a + 1, :]
                right = corner[2 * SUB + first + 2 + a : 2 * SUB + first + 3 + a, :]
                out.append(jnp.where(index == 0, sign * left, jnp.where(index == 1, sign * right, 0.0)))
            return out + [zero] * (newest - 2)

        blk_stat = pick(0, 1.0)
        blk_spec = pick(4, -1.0)
    else:
        blk_stat = [blocks_in[0][b] for b in range(newest)]
        blk_spec = [blocks_in[1][b] for b in range(newest)]
    tadpole = corner[3 * SUB : 3 * SUB + 1, :]
    momentum = momentum[place[0]]
    frequency = momentum * momentum + MASS_SQUARED + HARTREE_COUPLING * tadpole

    total_stat = extra[0, 0:SUB, :]
    total_spec = extra[0, SUB : 2 * SUB, :]
    for g in range(1, groups):
        total_stat += extra[g, 0:SUB, :]
        total_spec += extra[g, SUB : 2 * SUB, :]
    memory_stat = mem_stat[...]
    memory_spec = mem_spec[...]
    for b in range(2, current + 1):
        weight_stat = own_ref[b : b + 1, :]
        weight_spec = own_ref[SUB + b : SUB + b + 1, :]
        memory_stat -= weight_spec * stats[b][...]
        memory_spec -= weight_spec * specs[b][...]
        total_stat -= weight_spec * blk_stat[b]
        total_stat += jnp.where(index >= b, weight_stat * blk_spec[b], 0.0)
        total_spec -= jnp.where(index <= b, weight_spec * blk_spec[b], 0.0)
    new_stat = (
        2.0 * stats[current][...]
        - stats[step][...]
        - factor * (frequency * stats[current][...] + TIME_STEP * memory_stat)
    )
    new_spec = (
        2.0 * specs[current][...]
        - specs[step][...]
        - factor * (frequency * specs[current][...] + TIME_STEP * memory_spec)
    )
    valid = index <= current
    line_stat = jnp.where(
        valid,
        2.0 * blk_stat[current]
        - blk_stat[step]
        - factor * (frequency * blk_stat[current] + TIME_STEP * total_stat),
        0.0,
    )
    line_spec = jnp.where(
        valid,
        2.0 * blk_spec[current]
        - blk_spec[step]
        - factor * (frequency * blk_spec[current] + TIME_STEP * total_spec),
        0.0,
    )
    diagonal = (
        2.0 * line_stat[current : current + 1]
        - line_stat[step : step + 1]
        - factor
        * (frequency * line_stat[current : current + 1] + TIME_STEP * total_stat[current : current + 1])
    )
    line_stat = jnp.where(index == current + 1, diagonal, line_stat)
    blk_stat[current + 1] = line_stat
    blk_spec[current + 1] = line_spec
    for b in range(newest):
        block_stat[b] = jnp.where(index == current + 1, line_stat[b : b + 1], blk_stat[b])
        block_spec[b] = jnp.where(index == current + 1, -line_spec[b : b + 1], blk_spec[b])
    if last_step:
        for b in range(2, newest - 1):
            rows_stat[b - 2] = stats[b][...]
            rows_spec[b - 2] = specs[b][...]
        rows_stat[newest - 3] = new_stat
        rows_spec[newest - 3] = new_spec
    else:
        next_stat_ref[...] = new_stat
        next_spec_ref[...] = new_spec
        half = rows + SUB
        out_ref[0:rows, :] = new_stat
        out_ref[half : half + rows, :] = new_spec
        out_ref[rows:half, :] = line_stat
        out_ref[half + rows :, :] = line_spec


def shards(history_stat, history_spec):
    rows, times, width = history_stat.shape
    history_stat = pltpu.with_memory_space_constraint(history_stat, pltpu.HBM)
    history_spec = pltpu.with_memory_space_constraint(history_spec, pltpu.HBM)
    newest = STEPS + 2
    half = rows + SUB
    hists, reps, moms = (lax.axis_size(a) for a in ("hist", "rep", "mom"))
    forward, backward, measure, momentum = tables(MOMENTA)
    forward = jnp.asarray(forward.reshape(moms, width, MOMENTA))
    backward = jnp.asarray(np.ascontiguousarray(backward.reshape(MOMENTA, moms, width).transpose(1, 0, 2)))
    measure = jnp.asarray(measure.reshape(moms, 1, width))
    own = lax.axis_index("mom")
    hist, rep = lax.axis_index("hist"), lax.axis_index("rep")
    momentum = jnp.asarray(momentum.reshape(moms, 1, width))
    place = jnp.stack([own, hist * reps + rep, jnp.int32(times - 1), hist, rep]).astype(jnp.int32)

    row_bytes = times * width * 4
    keep = min(2 * rows, RESIDENT_BYTES // row_bytes // SUB * SUB)
    keep_stat = rows
    keep_spec = keep - rows
    split = PART_ROWS
    sizes_stat = [(r, min(split, keep_stat - r)) for r in range(0, keep_stat, split)]
    sizes_spec = [(r, min(split, keep_spec - r)) for r in range(0, keep_spec, split)]
    stream = (keep_spec // SUB,) if keep_spec < rows else None

    c0, c1, d0, d1, send = pl.pallas_call(
        first_kernel,
        in_specs=[HBM] * 2,
        out_specs=[VMEM] * 5,
        out_shape=[jax.ShapeDtypeStruct((rows, width), F32)] * 4
        + [jax.ShapeDtypeStruct((2 * half, width), F32)],
        scratch_shapes=[pltpu.VMEM((rows, SUB, width), F32)] * 2 + [pltpu.SemaphoreType.DMA((2,))],
        compiler_params=params(3),
        name="first",
    )(history_stat, history_spec)
    stats, specs = [c0, c1], [d0, d1]
    blocks = ()
    for step in range(STEPS):
        pieces = [send] + [lax.ppermute(send, "mom", shifts(moms, k)) for k in range(1, moms)]
        z, own_rows = pl.pallas_call(
            functools.partial(transform_kernel, step, moms),
            in_specs=[SMEM] + [VMEM] * (moms + 3 + len(stats) + len(specs)),
            out_specs=[VMEM] * 2,
            out_shape=[
                jax.ShapeDtypeStruct((2 * rows + EXTRA, width), F32),
                jax.ShapeDtypeStruct((2 * SUB, width), F32),
            ],
            compiler_params=params(6),
            name=f"transform_{step}",
        )(place, *pieces, forward, backward, measure, *stats, *specs)
        along = [z] + [lax.ppermute(z, "hist", shifts(hists, k)) for k in range(1, hists)]
        if step == 0:
            sources = [history_stat] * len(sizes_stat) + [history_spec] * len(sizes_spec)
            kept = [load([a], [n], z)[0] for a, n in zip(sources, sizes_stat + sizes_spec)]
        gathered = []
        for piece in along:
            gathered += [piece] + [lax.ppermute(piece, "rep", shifts(reps, q)) for q in range(1, reps)]
        last = step == STEPS - 1
        block_shape = jax.ShapeDtypeStruct((newest, SUB, width), F32)
        row_shape = jax.ShapeDtypeStruct((rows, width), F32)
        if last:
            out_shape = [jax.ShapeDtypeStruct((STEPS, rows, width), F32)] * 2 + [block_shape] * 2
        else:
            out_shape = [row_shape] * 2 + [block_shape] * 2
            out_shape += [jax.ShapeDtypeStruct((2 * half, width), F32)]
        scratch = [pltpu.VMEM((times, width), F32)] * 2 + [
            pltpu.VMEM((hists * reps, EXTRA, width), F32),
            pltpu.VMEM((rows, width), F32),
            pltpu.VMEM((rows, width), F32),
        ]
        operands = [*gathered, own_rows, momentum, *stats, *specs, *blocks, *kept]
        in_specs = [SMEM] + [VMEM] * len(operands)
        if stream:
            operands.append(history_spec)
            in_specs.append(HBM)
            scratch += [pltpu.VMEM((2, SUB, times, width), F32), pltpu.SemaphoreType.DMA((2,))]
        outs = pl.pallas_call(
            functools.partial(
                memory_kernel, step, (hists, reps), (sizes_stat, sizes_spec), stream
            ),
            in_specs=in_specs,
            out_specs=[VMEM] * len(out_shape),
            out_shape=out_shape,
            scratch_shapes=scratch,
            compiler_params=params(11),
            name=f"memory_{step}",
        )(place, *operands)
        if last:
            return outs[0], outs[1], outs[2][:, :newest], outs[3][:, :newest]
        stats.append(outs[0])
        specs.append(outs[1])
        blocks = (outs[2], outs[3])
        send = outs[4]


def solution(mesh):
    in_specs = (P(("hist", "rep"), "ens", "mom"), P(("hist", "rep"), "ens", "mom"))
    out_specs = (
        P("ens", ("hist", "rep"), "mom"),
        P("ens", ("hist", "rep"), "mom"),
        P("ens", None, "mom"),
        P("ens", None, "mom"),
    )
    return jax.shard_map(shards, mesh=mesh, in_specs=in_specs, out_specs=out_specs, check_vma=False)
```

profile of v0, /device:TPU:0, one launch (start us, length us, event | category | flops | bytes accessed | tf_op | source)
XLA Modules:
  0.0 138.8 jit_solution(7878955635076296699)
XLA Ops:
  2.2 3.0 %collective-permute-start = (f32[144,256]{1,0:T(8,128)S(1)}, f32[144,256]{1,0:T(8,128)S(1)}, u32[]{:S(2)}, u32[]{:S(2)}) collective-permute-start(f32[144,256]{1,0:T(8,128)S(1)} %get-tuple-element.29.refs_1_), channel_id=1, source_target_pairs={{0,2},{2,0},{1,3},{3,1},{4,6},{6,4},{5,7},{7,5},{8,10},{10,8},{9,1... | collective-permute-start | bytes 442376 | tf_op jit(solution)/shard_map/ppermute | solution.py:402
  5.3 3.8 %collective-permute-done.refs_2_ = f32[144,256]{1,0:T(8,128)S(1)} collective-permute-done((f32[144,256]{1,0:T(8,128)S(1)}, f32[144,256]{1,0:T(8,128)S(1)}, u32[]{:S(2)}, u32[]{:S(2)}) %collective-permute-start) | collective-permute-done | bytes 147488 | tf_op jit(solution)/shard_map/ppermute | solution.py:402
  9.1 1.9 %transform_0.1 = (f32[160,256]{1,0:T(8,128)S(1)}, f32[16,256]{1,0:T(8,128)S(1)}) custom-call(s32[5]{0:T(128)S(1)} %stack.19.refs_0_, f32[144,256]{1,0:T(8,128)S(1)} %get-tuple-element.29.refs_1_, f32[144,256]{1,0:T(8,128)S(1)} %collective-permute-done.refs_2_, f32[2,256,512]{2,1,0:T(8,128)S(1)} %copy-done.1, f32[2,512,256]{2,1,0:T(8,128)S(1)} %copy-done, ...), custom_call_target="tpu_custom_call" | custom-call | tf_op jit(solution)/shard_map/transform_0/pallas_call | solution.py:403
  11.0 3.9 %collective-permute-start.6 = (f32[160,256]{1,0:T(8,128)S(1)}, f32[160,256]{1,0:T(8,128)S(1)}, u32[]{:S(2)}, u32[]{:S(2)}) collective-permute-start(f32[160,256]{1,0:T(8,128)S(1)} %get-tuple-element.34.refs_1_), channel_id=1, source_target_pairs={{0,12},{4,0},{8,4},{12,8},{1,13},{5,1},{9,5},{13,9},{2,14},{6,2},{... | collective-permute-start | bytes 491528 | tf_op jit(solution)/shard_map/ppermute | solution.py:414
  15.9 3.6 %collective-permute-done.6.refs_7_ = f32[160,256]{1,0:T(8,128)S(1)} collective-permute-done((f32[160,256]{1,0:T(8,128)S(1)}, f32[160,256]{1,0:T(8,128)S(1)}, u32[]{:S(2)}, u32[]{:S(2)}) %collective-permute-start.6) | collective-permute-done | bytes 163872 | tf_op jit(solution)/shard_map/ppermute | solution.py:414
  19.5 8.7 %collective-permute-done.4.refs_5_ = f32[160,256]{1,0:T(8,128)S(1)} collective-permute-done((f32[160,256]{1,0:T(8,128)S(1)}, f32[160,256]{1,0:T(8,128)S(1)}, u32[]{:S(2)}, u32[]{:S(2)}) %collective-permute-start.4) | collective-permute-done | bytes 163872 | tf_op jit(solution)/shard_map/ppermute | solution.py:414
  28.7 3.4 %load.9.refs_19_.refs_23_.refs_25_ = f32[16,512,256]{2,1,0:T(8,128)S(1)} custom-call(f32[64,512,256]{2,1,0:T(8,128)} %refs_26_.1, f32[160,256]{1,0:T(8,128)S(1)} %get-tuple-element.34.refs_1_), custom_call_target="tpu_custom_call" | custom-call | tf_op jit(solution)/shard_map/load/pallas_call | solution.py:90
  32.1 3.4 %load.8.refs_18_.refs_22_.refs_24_ = f32[16,512,256]{2,1,0:T(8,128)S(1)} custom-call(f32[64,512,256]{2,1,0:T(8,128)} %refs_0_.8, f32[160,256]{1,0:T(8,128)S(1)} %get-tuple-element.34.refs_1_), custom_call_target="tpu_custom_call" | custom-call | tf_op jit(solution)/shard_map/load/pallas_call | solution.py:90
  35.5 3.4 %load.7.refs_17_.refs_21_.refs_23_ = f32[16,512,256]{2,1,0:T(8,128)S(1)} custom-call(f32[64,512,256]{2,1,0:T(8,128)} %refs_0_.8, f32[160,256]{1,0:T(8,128)S(1)} %get-tuple-element.34.refs_1_), custom_call_target="tpu_custom_call" | custom-call | tf_op jit(solution)/shard_map/load/pallas_call | solution.py:90
  38.9 3.4 %load.6.refs_16_.refs_20_.refs_22_ = f32[16,512,256]{2,1,0:T(8,128)S(1)} custom-call(f32[64,512,256]{2,1,0:T(8,128)} %refs_0_.8, f32[160,256]{1,0:T(8,128)S(1)} %get-tuple-element.34.refs_1_), custom_call_target="tpu_custom_call" | custom-call | tf_op jit(solution)/shard_map/load/pallas_call | solution.py:90
  42.3 3.4 %load.5.refs_15_.refs_19_.refs_21_ = f32[16,512,256]{2,1,0:T(8,128)S(1)} custom-call(f32[64,512,256]{2,1,0:T(8,128)} %refs_0_.8, f32[160,256]{1,0:T(8,128)S(1)} %get-tuple-element.34.refs_1_), custom_call_target="tpu_custom_call" | custom-call | tf_op jit(solution)/shard_map/load/pallas_call | solution.py:90
  45.7 13.6 %memory_0.1 = (f32[64,256]{1,0:T(8,128)S(1)}, f32[64,256]{1,0:T(8,128)S(1)}, f32[5,8,256]{2,1,0:T(8,128)S(1)}, f32[5,8,256]{2,1,0:T(8,128)S(1)}, f32[144,256]{1,0:T(8,128)S(1)}) custom-call(s32[5]{0:T(128)S(1)} %stack.19.refs_0_, f32[160,256]{1,0:T(8,128)S(1)} %get-tuple-element.34.refs_1_, f32[160,256]{1,0:T(8,128)S(1)} %collective-permute-done.1.refs_2_, ...), custom_call_target="tpu_custom_call" | custom-call | tf_op jit(solution)/shard_map/memory_0/pallas_call | solution.py:440
  60.9 4.3 %collective-permute-done.8.refs_2_ = f32[144,256]{1,0:T(8,128)S(1)} collective-permute-done((f32[144,256]{1,0:T(8,128)S(1)}, f32[144,256]{1,0:T(8,128)S(1)}, u32[]{:S(2)}, u32[]{:S(2)}) %collective-permute-start.8) | collective-permute-done | bytes 147488 | tf_op jit(solution)/shard_map/ppermute | solution.py:402
  65.2 1.9 %transform_1.1 = (f32[160,256]{1,0:T(8,128)S(1)}, f32[16,256]{1,0:T(8,128)S(1)}) custom-call(s32[5]{0:T(128)S(1)} %stack.19.refs_0_, f32[144,256]{1,0:T(8,128)S(1)} %get-tuple-element.36.refs_1_, f32[144,256]{1,0:T(8,128)S(1)} %collective-permute-done.8.refs_2_, f32[2,256,512]{2,1,0:T(8,128)S(1)} %copy-done.1, f32[2,512,256]{2,1,0:T(8,128)S(1)} %copy-done, ...), custom_call_target="tpu_custom_call" | custom-call | tf_op jit(solution)/shard_map/transform_1/pallas_call | solution.py:403
  68.3 1.8 %collective-permute-start.12 = (f32[160,256]{1,0:T(8,128)S(1)}, f32[160,256]{1,0:T(8,128)S(1)}, u32[]{:S(2)}, u32[]{:S(2)}) collective-permute-start(f32[160,256]{1,0:T(8,128)S(1)} %get-tuple-element.39.refs_1_), channel_id=1, source_target_pairs={{0,8},{4,12},{8,0},{12,4},{1,9},{5,13},{9,1},{13,5},{2,10},{6,14},... | collective-permute-start | bytes 491528 | tf_op jit(solution)/shard_map/ppermute | solution.py:414
  70.1 1.9 %collective-permute-start.10 = (f32[160,256]{1,0:T(8,128)S(1)}, f32[160,256]{1,0:T(8,128)S(1)}, u32[]{:S(2)}, u32[]{:S(2)}) collective-permute-start(f32[160,256]{1,0:T(8,128)S(1)} %get-tuple-element.39.refs_1_), channel_id=1, source_target_pairs={{0,4},{4,8},{8,12},{12,0},{1,5},{5,9},{9,13},{13,1},{2,6},{6,10},{... | collective-permute-start | bytes 491528 | tf_op jit(solution)/shard_map/ppermute | solution.py:414
  72.6 12.0 %collective-permute-done.12.refs_5_ = f32[160,256]{1,0:T(8,128)S(1)} collective-permute-done((f32[160,256]{1,0:T(8,128)S(1)}, f32[160,256]{1,0:T(8,128)S(1)}, u32[]{:S(2)}, u32[]{:S(2)}) %collective-permute-start.12) | collective-permute-done | bytes 163872 | tf_op jit(solution)/shard_map/ppermute | solution.py:414
  86.2 13.6 %memory_1.1 = (f32[64,256]{1,0:T(8,128)S(1)}, f32[64,256]{1,0:T(8,128)S(1)}, f32[5,8,256]{2,1,0:T(8,128)S(1)}, f32[5,8,256]{2,1,0:T(8,128)S(1)}, f32[144,256]{1,0:T(8,128)S(1)}) custom-call(s32[5]{0:T(128)S(1)} %stack.19.refs_0_, f32[160,256]{1,0:T(8,128)S(1)} %get-tuple-element.39.refs_1_, f32[160,256]{1,0:T(8,128)S(1)} %collective-permute-done.9.refs_2_, ...), custom_call_target="tpu_custom_call" | custom-call | tf_op jit(solution)/shard_map/memory_1/pallas_call | solution.py:440
  101.4 4.6 %collective-permute-done.16.refs_2_ = f32[144,256]{1,0:T(8,128)S(1)} collective-permute-done((f32[144,256]{1,0:T(8,128)S(1)}, f32[144,256]{1,0:T(8,128)S(1)}, u32[]{:S(2)}, u32[]{:S(2)}) %collective-permute-start.16) | collective-permute-done | bytes 147488 | tf_op jit(solution)/shard_map/ppermute | solution.py:402
  106.0 2.0 %transform_2.1 = (f32[160,256]{1,0:T(8,128)S(1)}, f32[16,256]{1,0:T(8,128)S(1)}) custom-call(s32[5]{0:T(128)S(1)} %stack.19.refs_0_, f32[144,256]{1,0:T(8,128)S(1)} %get-tuple-element.43.refs_1_, f32[144,256]{1,0:T(8,128)S(1)} %collective-permute-done.16.refs_2_, f32[2,256,512]{2,1,0:T(8,128)S(1)} %copy-done.1, f32[2,512,256]{2,1,0:T(8,128)S(1)} %copy-done, ...), custom_call_target="tpu_custom_call" | custom-call | tf_op jit(solution)/shard_map/transform_2/pallas_call | solution.py:403
  108.4 1.9 %collective-permute-start.18 = (f32[160,256]{1,0:T(8,128)S(1)}, f32[160,256]{1,0:T(8,128)S(1)}, u32[]{:S(2)}, u32[]{:S(2)}) collective-permute-start(f32[160,256]{1,0:T(8,128)S(1)} %get-tuple-element.46.refs_1_), channel_id=1, source_target_pairs={{0,4},{4,8},{8,12},{12,0},{1,5},{5,9},{9,13},{13,1},{2,6},{6,10},{... | collective-permute-start | bytes 491528 | tf_op jit(solution)/shard_map/ppermute | solution.py:414
  110.3 4.5 %collective-permute-done.22.refs_7_ = f32[160,256]{1,0:T(8,128)S(1)} collective-permute-done((f32[160,256]{1,0:T(8,128)S(1)}, f32[160,256]{1,0:T(8,128)S(1)}, u32[]{:S(2)}, u32[]{:S(2)}) %collective-permute-start.22) | collective-permute-done | bytes 163872 | tf_op jit(solution)/shard_map/ppermute | solution.py:414
  114.9 7.7 %collective-permute-done.20.refs_5_ = f32[160,256]{1,0:T(8,128)S(1)} collective-permute-done((f32[160,256]{1,0:T(8,128)S(1)}, f32[160,256]{1,0:T(8,128)S(1)}, u32[]{:S(2)}, u32[]{:S(2)}) %collective-permute-start.20) | collective-permute-done | bytes 163872 | tf_op jit(solution)/shard_map/ppermute | solution.py:414
  124.2 14.5 %memory_2.1 = (f32[3,64,256]{2,1,0:T(8,128)}, f32[3,64,256]{2,1,0:T(8,128)}, f32[5,8,256]{2,1,0:T(8,128)}, f32[5,8,256]{2,1,0:T(8,128)}) custom-call(s32[5]{0:T(128)S(1)} %stack.19.refs_0_, f32[160,256]{1,0:T(8,128)S(1)} %get-tuple-element.46.refs_1_, f32[160,256]{1,0:T(8,128)S(1)} %collective-permute-done.17.refs_2_, ...), custom_call_target="tpu_custom_call" | custom-call | tf_op jit(solution)/shard_map/memory_2/pallas_call | solution.py:440
  (45 shorter events, 11.6 us)
Async XLA Ops:
  2.2 6.9 %collective-permute-start = (f32[144,256]{1,0:T(8,128)S(1)}, f32[144,256]{1,0:T(8,128)S(1)}, u32[]{:S(2)}, u32[]{:S(2)}) collective-permute-start(f32[144,256]{1,0:T(8,128)S(1)} %get-tuple-element.29.refs_1_), channel_id=1, source_target_pairs={{0,2},{2,0},{1,3},{3,1},{4,6},{6,4},{5,7},{7,5},{8,10},{10,8},{9,1... | collective-permute-start | bytes 442376 | tf_op jit(solution)/shard_map/ppermute | solution.py:402
  11.0 8.5 %collective-permute-start.6 = (f32[160,256]{1,0:T(8,128)S(1)}, f32[160,256]{1,0:T(8,128)S(1)}, u32[]{:S(2)}, u32[]{:S(2)}) collective-permute-start(f32[160,256]{1,0:T(8,128)S(1)} %get-tuple-element.34.refs_1_), channel_id=1, source_target_pairs={{0,12},{4,0},{8,4},{12,8},{1,13},{5,1},{9,5},{13,9},{2,14},{6,2},{... | collective-permute-start | bytes 491528 | tf_op jit(solution)/shard_map/ppermute | solution.py:414
  14.9 13.3 %collective-permute-start.4 = (f32[160,256]{1,0:T(8,128)S(1)}, f32[160,256]{1,0:T(8,128)S(1)}, u32[]{:S(2)}, u32[]{:S(2)}) collective-permute-start(f32[160,256]{1,0:T(8,128)S(1)} %get-tuple-element.34.refs_1_), channel_id=1, source_target_pairs={{0,8},{4,12},{8,0},{12,4},{1,9},{5,13},{9,1},{13,5},{2,10},{6,14},... | collective-permute-start | bytes 491528 | tf_op jit(solution)/shard_map/ppermute | solution.py:414
  14.9 13.3 %collective-permute-start.2 = (f32[160,256]{1,0:T(8,128)S(1)}, f32[160,256]{1,0:T(8,128)S(1)}, u32[]{:S(2)}, u32[]{:S(2)}) collective-permute-start(f32[160,256]{1,0:T(8,128)S(1)} %get-tuple-element.34.refs_1_), channel_id=1, source_target_pairs={{0,4},{4,8},{8,12},{12,0},{1,5},{5,9},{9,13},{13,1},{2,6},{6,10},{... | collective-permute-start | bytes 491528 | tf_op jit(solution)/shard_map/ppermute | solution.py:414
  15.9 29.8 %collective-permute-start.1 = (f32[160,256]{1,0:T(8,128)S(1)}, f32[160,256]{1,0:T(8,128)S(1)}, u32[]{:S(2)}, u32[]{:S(2)}) collective-permute-start(f32[160,256]{1,0:T(8,128)S(1)} %get-tuple-element.34.refs_1_), channel_id=1, source_target_pairs={{0,1},{1,0},{2,3},{3,2},{4,5},{5,4},{6,7},{7,6},{8,9},{9,8},{10,11... | collective-permute-start | bytes 491528 | tf_op jit(solution)/shard_map/ppermute | solution.py:420
  19.5 26.2 %collective-permute-start.7 = (f32[160,256]{1,0:T(8,128)S(1)}, f32[160,256]{1,0:T(8,128)S(1)}, u32[]{:S(2)}, u32[]{:S(2)}) collective-permute-start(f32[160,256]{1,0:T(8,128)S(1)} %collective-permute-done.6.refs_7_), channel_id=1, source_target_pairs={{0,1},{1,0},{2,3},{3,2},{4,5},{5,4},{6,7},{7,6},{8,9},{9,8},{10,11... | collective-permute-start | bytes 491528 | tf_op jit(solution)/shard_map/ppermute | solution.py:420
  28.2 17.6 %collective-permute-start.5 = (f32[160,256]{1,0:T(8,128)S(1)}, f32[160,256]{1,0:T(8,128)S(1)}, u32[]{:S(2)}, u32[]{:S(2)}) collective-permute-start(f32[160,256]{1,0:T(8,128)S(1)} %collective-permute-done.4.refs_5_), channel_id=1, source_target_pairs={{0,1},{1,0},{2,3},{3,2},{4,5},{5,4},{6,7},{7,6},{8,9},{9,8},{10,11... | collective-permute-start | bytes 491528 | tf_op jit(solution)/shard_map/ppermute | solution.py:420
  28.2 17.6 %collective-permute-start.3 = (f32[160,256]{1,0:T(8,128)S(1)}, f32[160,256]{1,0:T(8,128)S(1)}, u32[]{:S(2)}, u32[]{:S(2)}) collective-permute-start(f32[160,256]{1,0:T(8,128)S(1)} %collective-permute-done.2.refs_3_), channel_id=1, source_target_pairs={{0,1},{1,0},{2,3},{3,2},{4,5},{5,4},{6,7},{7,6},{8,9},{9,8},{10,11... | collective-permute-start | bytes 491528 | tf_op jit(solution)/shard_map/ppermute | solution.py:420
  59.4 5.9 %collective-permute-start.8 = (f32[144,256]{1,0:T(8,128)S(1)}, f32[144,256]{1,0:T(8,128)S(1)}, u32[]{:S(2)}, u32[]{:S(2)}) collective-permute-start(f32[144,256]{1,0:T(8,128)S(1)} %get-tuple-element.36.refs_1_), channel_id=1, source_target_pairs={{0,2},{2,0},{1,3},{3,1},{4,6},{6,4},{5,7},{7,5},{8,10},{10,8},{9,1... | collective-permute-start | bytes 442376 | tf_op jit(solution)/shard_map/ppermute | solution.py:402
  67.2 5.4 %collective-permute-start.14 = (f32[160,256]{1,0:T(8,128)S(1)}, f32[160,256]{1,0:T(8,128)S(1)}, u32[]{:S(2)}, u32[]{:S(2)}) collective-permute-start(f32[160,256]{1,0:T(8,128)S(1)} %get-tuple-element.39.refs_1_), channel_id=1, source_target_pairs={{0,12},{4,0},{8,4},{12,8},{1,13},{5,1},{9,5},{13,9},{2,14},{6,2},{... | collective-permute-start | bytes 491528 | tf_op jit(solution)/shard_map/ppermute | solution.py:414
  68.3 16.3 %collective-permute-start.12 = (f32[160,256]{1,0:T(8,128)S(1)}, f32[160,256]{1,0:T(8,128)S(1)}, u32[]{:S(2)}, u32[]{:S(2)}) collective-permute-start(f32[160,256]{1,0:T(8,128)S(1)} %get-tuple-element.39.refs_1_), channel_id=1, source_target_pairs={{0,8},{4,12},{8,0},{12,4},{1,9},{5,13},{9,1},{13,5},{2,10},{6,14},... | collective-permute-start | bytes 491528 | tf_op jit(solution)/shard_map/ppermute | solution.py:414
  70.1 14.5 %collective-permute-start.10 = (f32[160,256]{1,0:T(8,128)S(1)}, f32[160,256]{1,0:T(8,128)S(1)}, u32[]{:S(2)}, u32[]{:S(2)}) collective-permute-start(f32[160,256]{1,0:T(8,128)S(1)} %get-tuple-element.39.refs_1_), channel_id=1, source_target_pairs={{0,4},{4,8},{8,12},{12,0},{1,5},{5,9},{9,13},{13,1},{2,6},{6,10},{... | collective-permute-start | bytes 491528 | tf_op jit(solution)/shard_map/ppermute | solution.py:414
  72.0 13.1 %collective-permute-start.9 = (f32[160,256]{1,0:T(8,128)S(1)}, f32[160,256]{1,0:T(8,128)S(1)}, u32[]{:S(2)}, u32[]{:S(2)}) collective-permute-start(f32[160,256]{1,0:T(8,128)S(1)} %get-tuple-element.39.refs_1_), channel_id=1, source_target_pairs={{0,1},{1,0},{2,3},{3,2},{4,5},{5,4},{6,7},{7,6},{8,9},{9,8},{10,11... | collective-permute-start | bytes 491528 | tf_op jit(solution)/shard_map/ppermute | solution.py:420
  72.6 12.5 %collective-permute-start.15 = (f32[160,256]{1,0:T(8,128)S(1)}, f32[160,256]{1,0:T(8,128)S(1)}, u32[]{:S(2)}, u32[]{:S(2)}) collective-permute-start(f32[160,256]{1,0:T(8,128)S(1)} %collective-permute-done.14.refs_7_), channel_id=1, source_target_pairs={{0,1},{1,0},{2,3},{3,2},{4,5},{5,4},{6,7},{7,6},{8,9},{9,8},{10,11... | collective-permute-start | bytes 491528 | tf_op jit(solution)/shard_map/ppermute | solution.py:420
  84.6 1.4 %collective-permute-start.13 = (f32[160,256]{1,0:T(8,128)S(1)}, f32[160,256]{1,0:T(8,128)S(1)}, u32[]{:S(2)}, u32[]{:S(2)}) collective-permute-start(f32[160,256]{1,0:T(8,128)S(1)} %collective-permute-done.12.refs_5_), channel_id=1, source_target_pairs={{0,1},{1,0},{2,3},{3,2},{4,5},{5,4},{6,7},{7,6},{8,9},{9,8},{10,11... | collective-permute-start | bytes 491528 | tf_op jit(solution)/shard_map/ppermute | solution.py:420
  84.6 1.6 %collective-permute-start.11 = (f32[160,256]{1,0:T(8,128)S(1)}, f32[160,256]{1,0:T(8,128)S(1)}, u32[]{:S(2)}, u32[]{:S(2)}) collective-permute-start(f32[160,256]{1,0:T(8,128)S(1)} %collective-permute-done.10.refs_3_), channel_id=1, source_target_pairs={{0,1},{1,0},{2,3},{3,2},{4,5},{5,4},{6,7},{7,6},{8,9},{9,8},{10,11... | collective-permute-start | bytes 491528 | tf_op jit(solution)/shard_map/ppermute | solution.py:420
  99.8 6.1 %collective-permute-start.16 = (f32[144,256]{1,0:T(8,128)S(1)}, f32[144,256]{1,0:T(8,128)S(1)}, u32[]{:S(2)}, u32[]{:S(2)}) collective-permute-start(f32[144,256]{1,0:T(8,128)S(1)} %get-tuple-element.43.refs_1_), channel_id=1, source_target_pairs={{0,2},{2,0},{1,3},{3,1},{4,6},{6,4},{5,7},{7,5},{8,10},{10,8},{9,1... | collective-permute-start | bytes 442376 | tf_op jit(solution)/shard_map/ppermute | solution.py:402
  107.9 6.9 %collective-permute-start.22 = (f32[160,256]{1,0:T(8,128)S(1)}, f32[160,256]{1,0:T(8,128)S(1)}, u32[]{:S(2)}, u32[]{:S(2)}) collective-permute-start(f32[160,256]{1,0:T(8,128)S(1)} %get-tuple-element.46.refs_1_), channel_id=1, source_target_pairs={{0,12},{4,0},{8,4},{12,8},{1,13},{5,1},{9,5},{13,9},{2,14},{6,2},{... | collective-permute-start | bytes 491528 | tf_op jit(solution)/shard_map/ppermute | solution.py:414
  108.0 14.5 %collective-permute-start.20 = (f32[160,256]{1,0:T(8,128)S(1)}, f32[160,256]{1,0:T(8,128)S(1)}, u32[]{:S(2)}, u32[]{:S(2)}) collective-permute-start(f32[160,256]{1,0:T(8,128)S(1)} %get-tuple-element.46.refs_1_), channel_id=1, source_target_pairs={{0,8},{4,12},{8,0},{12,4},{1,9},{5,13},{9,1},{13,5},{2,10},{6,14},... | collective-permute-start | bytes 491528 | tf_op jit(solution)/shard_map/ppermute | solution.py:414
  108.4 14.2 %collective-permute-start.18 = (f32[160,256]{1,0:T(8,128)S(1)}, f32[160,256]{1,0:T(8,128)S(1)}, u32[]{:S(2)}, u32[]{:S(2)}) collective-permute-start(f32[160,256]{1,0:T(8,128)S(1)} %get-tuple-element.46.refs_1_), channel_id=1, source_target_pairs={{0,4},{4,8},{8,12},{12,0},{1,5},{5,9},{9,13},{13,1},{2,6},{6,10},{... | collective-permute-start | bytes 491528 | tf_op jit(solution)/shard_map/ppermute | solution.py:414
  110.3 12.7 %collective-permute-start.17 = (f32[160,256]{1,0:T(8,128)S(1)}, f32[160,256]{1,0:T(8,128)S(1)}, u32[]{:S(2)}, u32[]{:S(2)}) collective-permute-start(f32[160,256]{1,0:T(8,128)S(1)} %get-tuple-element.46.refs_1_), channel_id=1, source_target_pairs={{0,1},{1,0},{2,3},{3,2},{4,5},{5,4},{6,7},{7,6},{8,9},{9,8},{10,11... | collective-permute-start | bytes 491528 | tf_op jit(solution)/shard_map/ppermute | solution.py:420
  114.9 8.2 %collective-permute-start.23 = (f32[160,256]{1,0:T(8,128)S(1)}, f32[160,256]{1,0:T(8,128)S(1)}, u32[]{:S(2)}, u32[]{:S(2)}) collective-permute-start(f32[160,256]{1,0:T(8,128)S(1)} %collective-permute-done.22.refs_7_), channel_id=1, source_target_pairs={{0,1},{1,0},{2,3},{3,2},{4,5},{5,4},{6,7},{7,6},{8,9},{9,8},{10,11... | collective-permute-start | bytes 491528 | tf_op jit(solution)/shard_map/ppermute | solution.py:420
  122.6 1.4 %collective-permute-start.21 = (f32[160,256]{1,0:T(8,128)S(1)}, f32[160,256]{1,0:T(8,128)S(1)}, u32[]{:S(2)}, u32[]{:S(2)}) collective-permute-start(f32[160,256]{1,0:T(8,128)S(1)} %collective-permute-done.20.refs_5_), channel_id=1, source_target_pairs={{0,1},{1,0},{2,3},{3,2},{4,5},{5,4},{6,7},{7,6},{8,9},{9,8},{10,11... | collective-permute-start | bytes 491528 | tf_op jit(solution)/shard_map/ppermute | solution.py:420
  122.6 1.6 %collective-permute-start.19 = (f32[160,256]{1,0:T(8,128)S(1)}, f32[160,256]{1,0:T(8,128)S(1)}, u32[]{:S(2)}, u32[]{:S(2)}) collective-permute-start(f32[160,256]{1,0:T(8,128)S(1)} %collective-permute-done.18.refs_3_), channel_id=1, source_target_pairs={{0,1},{1,0},{2,3},{3,2},{4,5},{5,4},{6,7},{7,6},{8,9},{9,8},{10,11... | collective-permute-start | bytes 491528 | tf_op jit(solution)/shard_map/ppermute | solution.py:420
  (4 other events, 28.7 us)
where the time goes:
time: 139 us
  Pallas kernels  66 us (47%)
  waiting for transfers between devices  51.9 us (37%)
  starting transfers between devices  19.8 us (14%)
    pallas_call x3, Pallas kernels, shards(): pl.pallas_call(functools.partial(memory_kernel, step, (hists, reps), (siz...  41.7 us
    ppermute x9, waiting for transfers between devices, shards(): lax.ppermute(z, 'hist', shifts(hists, k))  37 us
    pallas_call x5, Pallas kernels, load(): pl.pallas_call(functools.partial(load_kernel, counts), out_shape=[pltpu.V...  17 us
    ppermute x3, waiting for transfers between devices, shards(): lax.ppermute(send, 'mom', shifts(moms, k))  12.7 us
    ppermute x9, starting transfers between devices, shards(): lax.ppermute(z, 'hist', shifts(hists, k))  12.1 us
    ppermute x3, starting transfers between devices, shards(): lax.ppermute(send, 'mom', shifts(moms, k))  6.15 us
    pallas_call x3, Pallas kernels, shards(): pl.pallas_call(functools.partial(transform_kernel, step, moms), in_specs=...  5.83 us
  transfers between devices with their start and end apart: 24, of which 13 were waited for; matrix products, arithmetic and copies ran while one was open for 0% of the time, Pallas kernels for 12%

commit v1 on v0

--- a/solution.py
+++ b/solution.py
@@ -8,6 +8,7 @@
 from jax.experimental import pallas as pl
 from jax.experimental.pallas import tpu as pltpu
 from jax.sharding import PartitionSpec as P
+
 
 MOMENTA = 512
 STEPS = 3
@@ -20,10 +21,17 @@
 
 SUB = 8
 LANES = 128
-WIDE = 32
+WIDE = 128
+PART = 32
+SLOTS = 4
 RESIDENT_BYTES = 40 * 2**20
 PART_ROWS = 16
-EXTRA = 32
+
+
+def extra_rows(step):
+    return 2 * SUB if step == 0 else SUB
+
+
 F32 = jnp.float32
 VMEM = pl.BlockSpec(memory_space=pltpu.VMEM)
 HBM = pl.BlockSpec(memory_space=pltpu.HBM)
@@ -134,26 +142,31 @@
     own_ref[0:SUB, :] = sigma[rows:half]
     own_ref[SUB : 2 * SUB, :] = sigma[half + rows :]
     row_times = times + lax.broadcasted_iota(jnp.int32, (rows, width), 0)
-    index = lax.broadcasted_iota(jnp.int32, (SUB, width), 0)
     base = 2 * rows
-    sums_stat = jnp.zeros((SUB, width), F32)
-    sums_spec = jnp.zeros((SUB, width), F32)
+    count = current + 1
+    lines = []
     last = place[2]
-    for a in range(current + 1):
-        column_stat = stats[a][...]
-        column_spec = specs[a][...]
+    for a in range(count):
         later = row_times <= last - 1 + a
+        partial = -group_spec * stats[a][...] - jnp.where(later, group_stat * specs[a][...], 0.0)
+        lines.append(jnp.sum(partial, axis=0, keepdims=True))
+    for a in range(2):
         earlier = row_times >= last - 1 + a
-        partial = -group_spec * column_stat - jnp.where(later, group_stat * column_spec, 0.0)
-        sums_stat = jnp.where(index == a, jnp.sum(partial, axis=0, keepdims=True), sums_stat)
-        partial = jnp.where(earlier, group_spec * column_spec, 0.0)
-        sums_spec = jnp.where(index == a, jnp.sum(partial, axis=0, keepdims=True), sums_spec)
-    out_ref[base : base + SUB, :] = sums_stat
-    out_ref[base + SUB : base + 2 * SUB, :] = sums_spec
-    out_ref[base + 2 * SUB : base + 3 * SUB, :] = jnp.concatenate(
-        [r[rows - 2 : rows, :] for r in (stats[0], stats[1], specs[0], specs[1])], axis=0
-    )
-    out_ref[base + 3 * SUB :, :] = jnp.broadcast_to(tadpole, (SUB, width))
+        partial = jnp.where(earlier, group_spec * specs[a][...], 0.0)
+        lines.append(jnp.sum(partial, axis=0, keepdims=True))
+    if step == 0:
+        lines += [r[rows - 2 : rows, :] for r in (stats[0], stats[1], specs[0], specs[1])]
+        lines.append(jnp.broadcast_to(tadpole, (1, width)))
+    used = sum(v.shape[0] for v in lines)
+    lines.append(jnp.zeros((extra_rows(step) - used, width), F32))
+    out_ref[base:, :] = jnp.concatenate([v for v in lines if v.shape[0]], axis=0)
+    own_ref[2 * SUB :, :] = jnp.broadcast_to(tadpole, (SUB, width))
+
+
+def stack_kernel(count, *refs):
+    out = refs[-1]
+    for i in range(count):
+        out[i] = refs[i][...]
 
 
 def memory_kernel(step, group_sizes, resident, stream, *refs):
@@ -169,7 +182,8 @@
         return head
 
     (place,) = take(1)
-    pieces = take(groups)
+    firsts = take(reps)
+    others = take(reps)
     (own_ref, momentum) = take(2)
     stats = take(current + 1)
     specs = take(current + 1)
@@ -191,16 +205,20 @@
     group = hist * reps + rep
     chunks = rows // SUB
 
-    def copy(c):
-        slot = (c - stream[0]) % 2
-        return pltpu.make_async_copy(hbm[0].at[pl.ds(c * SUB, SUB)], buffers.at[slot], sem.at[slot])
-
-    if stream:
-        for c in range(stream[0], min(stream[0] + 2, chunks)):
-            copy(c).start()
+    parts = width // LANES
+    units = (chunks - stream[0]) * parts if stream else 0
+
+    def copy(unit):
+        at = pl.multiple_of((stream[0] + unit // parts) * SUB, SUB)
+        lane = pl.multiple_of((unit % parts) * LANES, LANES)
+        source = hbm[0].at[pl.ds(at, SUB), :, pl.ds(lane, LANES)]
+        return pltpu.make_async_copy(source, buffers.at[unit % SLOTS], sem.at[unit % SLOTS])
+
+    for unit in range(min(SLOTS, units)):
+        copy(jnp.int32(unit)).start()
     for k in range(hists):
         for q in range(reps):
-            piece = pieces[k * reps + q]
+            piece = firsts[q] if k == 0 else others[q].at[k - 1]
             who = lax.rem(hist + (hists - k), hists) * reps + lax.rem(rep + (reps - q), reps)
             at = pl.multiple_of(who * rows, SUB)
             sig_stat[pl.ds(at, rows), :] = piece[0:rows, :]
@@ -214,62 +232,76 @@
                 return ref, start - first
         return None, 0
 
-    tile = lax.broadcasted_iota(jnp.int32, (SUB, LANES), 0)
     for c in range(chunks):
         stat_ref, stat_at = find(stat_parts, resident[0], c)
         spec_ref, spec_at = find(spec_parts, resident[1], c)
-        if spec_ref is None:
-            copy(c).wait()
-            spec_ref, spec_at = buffers.at[(c - stream[0]) % 2], 0
-        first_time = group * rows + c * SUB
-        middle = first_time // WIDE
-        for l in range(width // LANES):
-            lane = slice(l * LANES, (l + 1) * LANES)
-
-            def below(j, acc, stat_ref=stat_ref, stat_at=stat_at, spec_ref=spec_ref, spec_at=spec_at, lane=lane):
+        streamed = spec_ref is None
+
+        def lanes(l, carry, c=c, stat_ref=stat_ref, stat_at=stat_at, spec_ref=spec_ref, spec_at=spec_at, streamed=streamed):
+            first_time = group * rows + c * SUB
+            middle = first_time // WIDE
+            lane = pl.ds(pl.multiple_of(l * LANES, LANES), LANES)
+            spec_lane = lane
+            if streamed:
+                unit = (c - stream[0]) * parts + l
+                copy(unit).wait()
+                spec_ref, spec_at = buffers.at[unit % SLOTS], 0
+                spec_lane = pl.ds(0, LANES)
+
+            def fold(value):
+                return jnp.sum(value.reshape(PART // SUB, SUB, LANES), axis=0)
+
+            def spans(j):
+                return [pl.ds(pl.multiple_of(j * WIDE + p, PART), PART) for p in range(0, WIDE, PART)]
+
+            def below(j, acc):
                 acc_stat, acc_spec = list(acc[0]), list(acc[1])
-                for t in range(WIDE // SUB):
-                    at = pl.ds(pl.multiple_of(j * WIDE + t * SUB, SUB), SUB)
+                for at in spans(j):
                     weight_stat, weight_spec = sig_stat[at, lane], sig_spec[at, lane]
                     for r in range(SUB):
-                        acc_stat[r] += weight_spec * stat_ref[stat_at + r, at, lane]
-                        acc_stat[r] += weight_stat * spec_ref[spec_at + r, at, lane]
+                        value = weight_spec * stat_ref[stat_at + r, at, lane]
+                        acc_stat[r] += fold(value + weight_stat * spec_ref[spec_at + r, at, spec_lane])
                 return tuple(acc_stat), tuple(acc_spec)
 
-            def above(j, acc, stat_ref=stat_ref, stat_at=stat_at, spec_ref=spec_ref, spec_at=spec_at, lane=lane):
+            def above(j, acc):
                 acc_stat, acc_spec = list(acc[0]), list(acc[1])
-                for t in range(WIDE // SUB):
-                    at = pl.ds(pl.multiple_of(j * WIDE + t * SUB, SUB), SUB)
+                for at in spans(j):
                     weight_spec = sig_spec[at, lane]
                     for r in range(SUB):
-                        acc_stat[r] += weight_spec * stat_ref[stat_at + r, at, lane]
-                        acc_spec[r] += weight_spec * spec_ref[spec_at + r, at, lane]
+                        acc_stat[r] += fold(weight_spec * stat_ref[stat_at + r, at, lane])
+                        acc_spec[r] += fold(weight_spec * spec_ref[spec_at + r, at, spec_lane])
                 return tuple(acc_stat), tuple(acc_spec)
 
-            zero = jnp.zeros((SUB, LANES), F32)
-            acc = (tuple(zero for _ in range(SUB)), tuple(zero for _ in range(SUB)))
+            def around(j, acc):
+                acc_stat, acc_spec = list(acc[0]), list(acc[1])
+                index = j * WIDE - first_time + lax.broadcasted_iota(jnp.int32, (PART, LANES), 0)
+                for p, at in enumerate(spans(j)):
+                    weight_stat, weight_spec = sig_stat[at, lane], sig_spec[at, lane]
+                    for r in range(SUB):
+                        early = index <= r - p * PART
+                        right = spec_ref[spec_at + r, at, spec_lane]
+                        value = weight_spec * stat_ref[stat_at + r, at, lane]
+                        acc_stat[r] += fold(value + jnp.where(early, weight_stat * right, 0.0))
+                        acc_spec[r] += fold(jnp.where(early, 0.0, weight_spec * right))
+                return tuple(acc_stat), tuple(acc_spec)
+
+            none = jnp.zeros((SUB, LANES), F32)
+            acc = (tuple(none for _ in range(SUB)), tuple(none for _ in range(SUB)))
             acc = lax.fori_loop(0, middle, below, acc)
-            acc_stat, acc_spec = list(acc[0]), list(acc[1])
-            for t in range(WIDE // SUB):
-                start = pl.multiple_of(middle * WIDE + t * SUB, SUB)
-                at = pl.ds(start, SUB)
-                weight_stat, weight_spec = sig_stat[at, lane], sig_spec[at, lane]
-                for r in range(SUB):
-                    value = spec_ref[spec_at + r, at, lane]
-                    early = start + tile <= first_time + r
-                    acc_stat[r] += weight_spec * stat_ref[stat_at + r, at, lane]
-                    acc_stat[r] += jnp.where(early, weight_stat * value, 0.0)
-                    acc_spec[r] += jnp.where(early, 0.0, weight_spec * value)
-            acc = (tuple(acc_stat), tuple(acc_spec))
+            acc = around(middle, acc)
             acc = lax.fori_loop(middle + 1, times // WIDE, above, acc)
-            mem_stat[c * SUB : (c + 1) * SUB, lane] = -jnp.concatenate(
-                [jnp.sum(a, axis=0, keepdims=True) for a in acc[0]], axis=0
-            )
-            mem_spec[c * SUB : (c + 1) * SUB, lane] = jnp.concatenate(
-                [jnp.sum(a, axis=0, keepdims=True) for a in acc[1]], axis=0
-            )
-        if stream and c >= stream[0] and c + 2 < chunks:
-            copy(c + 2).start()
+            here = pl.ds(c * SUB, SUB)
+            mem_stat[here, lane] = -jnp.concatenate([jnp.sum(a, axis=0, keepdims=True) for a in acc[0]], axis=0)
+            mem_spec[here, lane] = jnp.concatenate([jnp.sum(a, axis=0, keepdims=True) for a in acc[1]], axis=0)
+            if streamed:
+
+                @pl.when(unit + SLOTS < units)
+                def _():
+                    copy(unit + SLOTS).start()
+
+            return carry
+
+        lax.fori_loop(0, width // LANES, lanes, 0)
 
     factor = TIME_STEP * TIME_STEP
     corner = extra[groups - 1]
@@ -279,25 +311,27 @@
         def pick(first, sign):
             out = []
             for a in range(2):
-                left = corner[2 * SUB + first + a : 2 * SUB + first + a + 1, :]
-                right = corner[2 * SUB + first + 2 + a : 2 * SUB + first + 3 + a, :]
+                left = corner[first + a : first + a + 1, :]
+                right = corner[first + 2 + a : first + 3 + a, :]
                 out.append(jnp.where(index == 0, sign * left, jnp.where(index == 1, sign * right, 0.0)))
             return out + [zero] * (newest - 2)
 
-        blk_stat = pick(0, 1.0)
-        blk_spec = pick(4, -1.0)
+        blk_stat = pick(4, 1.0)
+        blk_spec = pick(8, -1.0)
+        tadpole = corner[12:13, :]
     else:
         blk_stat = [blocks_in[0][b] for b in range(newest)]
         blk_spec = [blocks_in[1][b] for b in range(newest)]
-    tadpole = corner[3 * SUB : 3 * SUB + 1, :]
+        tadpole = own_ref[2 * SUB : 2 * SUB + 1, :]
     momentum = momentum[place[0]]
     frequency = momentum * momentum + MASS_SQUARED + HARTREE_COUPLING * tadpole
 
-    total_stat = extra[0, 0:SUB, :]
-    total_spec = extra[0, SUB : 2 * SUB, :]
+    total = extra[0]
     for g in range(1, groups):
-        total_stat += extra[g, 0:SUB, :]
-        total_spec += extra[g, SUB : 2 * SUB, :]
+        total += extra[g]
+    count = current + 1
+    total_stat = jnp.concatenate([total[:count], jnp.zeros((SUB - count, width), F32)], axis=0)
+    total_spec = jnp.concatenate([total[count : count + 2], jnp.zeros((SUB - 2, width), F32)], axis=0)
     memory_stat = mem_stat[...]
     memory_spec = mem_spec[...]
     for b in range(2, current + 1):
@@ -399,25 +433,38 @@
     stats, specs = [c0, c1], [d0, d1]
     blocks = ()
     for step in range(STEPS):
-        pieces = [send] + [lax.ppermute(send, "mom", shifts(moms, k)) for k in range(1, moms)]
+        pieces = [send]
+        for k in range(1, moms):
+            pieces.append(lax.ppermute(send, "mom", shifts(moms, k)))
         z, own_rows = pl.pallas_call(
             functools.partial(transform_kernel, step, moms),
             in_specs=[SMEM] + [VMEM] * (moms + 3 + len(stats) + len(specs)),
             out_specs=[VMEM] * 2,
             out_shape=[
-                jax.ShapeDtypeStruct((2 * rows + EXTRA, width), F32),
-                jax.ShapeDtypeStruct((2 * SUB, width), F32),
+                jax.ShapeDtypeStruct((2 * rows + extra_rows(step), width), F32),
+                jax.ShapeDtypeStruct((3 * SUB, width), F32),
             ],
             compiler_params=params(6),
-            name=f"transform_{step}",
         )(place, *pieces, forward, backward, measure, *stats, *specs)
-        along = [z] + [lax.ppermute(z, "hist", shifts(hists, k)) for k in range(1, hists)]
+        along = []
+        for k in range(1, hists):
+            along.append(lax.ppermute(z, "hist", shifts(hists, k)))
+        firsts = [z] + [lax.ppermute(z, "rep", shifts(reps, q)) for q in range(1, reps)]
         if step == 0:
             sources = [history_stat] * len(sizes_stat) + [history_spec] * len(sizes_spec)
-            kept = [load([a], [n], z)[0] for a, n in zip(sources, sizes_stat + sizes_spec)]
-        gathered = []
-        for piece in along:
-            gathered += [piece] + [lax.ppermute(piece, "rep", shifts(reps, q)) for q in range(1, reps)]
+            kept = []
+            for source, count in zip(sources, sizes_stat + sizes_spec):
+                kept += load([source], [count], z)
+        other = pl.pallas_call(
+            functools.partial(stack_kernel, hists - 1),
+            in_specs=[VMEM] * (hists - 1),
+            out_specs=VMEM,
+            out_shape=jax.ShapeDtypeStruct((hists - 1,) + z.shape, F32),
+            compiler_params=params(2),
+            name="stack",
+        )(*along)
+        others = [other] + [lax.ppermute(other, "rep", shifts(reps, q)) for q in range(1, reps)]
+        gathered = firsts + others
         last = step == STEPS - 1
         block_shape = jax.ShapeDtypeStruct((newest, SUB, width), F32)
         row_shape = jax.ShapeDtypeStruct((rows, width), F32)
@@ -427,7 +474,7 @@
             out_shape = [row_shape] * 2 + [block_shape] * 2
             out_shape += [jax.ShapeDtypeStruct((2 * half, width), F32)]
         scratch = [pltpu.VMEM((times, width), F32)] * 2 + [
-            pltpu.VMEM((hists * reps, EXTRA, width), F32),
+            pltpu.VMEM((hists * reps, extra_rows(step), width), F32),
             pltpu.VMEM((rows, width), F32),
             pltpu.VMEM((rows, width), F32),
         ]
@@ -436,7 +483,7 @@
         if stream:
             operands.append(history_spec)
             in_specs.append(HBM)
-            scratch += [pltpu.VMEM((2, SUB, times, width), F32), pltpu.SemaphoreType.DMA((2,))]
+            scratch += [pltpu.VMEM((SLOTS, SUB, times, LANES), F32), pltpu.SemaphoreType.DMA((SLOTS,))]
         outs = pl.pallas_call(
             functools.partial(
                 memory_kernel, step, (hists, reps), (sizes_stat, sizes_spec), stream
@@ -446,7 +493,6 @@
             out_shape=out_shape,
             scratch_shapes=scratch,
             compiler_params=params(11),
-            name=f"memory_{step}",
         )(place, *operands)
         if last:
             return outs[0], outs[1], outs[2][:, :newest], outs[3][:, :newest]

time: 139 us -> 122 us (0.88)
  Pallas kernels: 66 us -> 53.9 us
  waiting for transfers between devices: 51.9 us -> 46.5 us
    pallas_call x3, Pallas kernels: 41.7 us -> 29.7 us  [shards(): pl.pallas_call(functools.partial(memory_kernel, step, (hists, reps), (siz...]
    ppermute x24 -> x18, waiting for transfers between devices: 51.9 us -> 46.5 us  [the longest x9 31.1 us: shards(): along.append(lax.ppermute(z, 'hist', shifts(hists, k)))]
    ppermute x24 -> x18, starting transfers between devices: 19.8 us -> 20.5 us  [the longest x9 12.6 us: shards(): along.append(lax.ppermute(z, 'hist', shifts(hists, k)))]
  transfers between devices with their start and end apart: 24 -> 18, of which waited for: 13 -> 11; matrix products, arithmetic and copies ran while one was open for 0% -> 0% of each run, Pallas kernels for 12% -> 14%
where the time goes in v1:
time: 122 us
  Pallas kernels  53.9 us (44%)
  waiting for transfers between devices  46.5 us (38%)
  starting transfers between devices  20.5 us (17%)
    ppermute x9, waiting for transfers between devices, shards(): along.append(lax.ppermute(z, 'hist', shifts(hists, k)))  31.1 us
    pallas_call x3, Pallas kernels, shards(): pl.pallas_call(functools.partial(memory_kernel, step, (hists, reps), (siz...  29.7 us
    pallas_call x5, Pallas kernels, load(): pl.pallas_call(functools.partial(load_kernel, counts), out_shape=[pltpu.V...  17 us
    ppermute x9, starting transfers between devices, shards(): along.append(lax.ppermute(z, 'hist', shifts(hists, k)))  12.6 us
    ppermute x3, waiting for transfers between devices, shards(): pieces.append(lax.ppermute(send, 'mom', shifts(moms, k)))  12.5 us
    ppermute x3, starting transfers between devices, shards(): pieces.append(lax.ppermute(send, 'mom', shifts(moms, k)))  6.14 us
    pallas_call x3, Pallas kernels, shards(): pl.pallas_call(functools.partial(transform_kernel, step, moms), in_specs=...  5.7 us
    ppermute x3, waiting for transfers between devices, shards(): lax.ppermute(z, 'rep', shifts(reps, q))  2.9 us
  transfers between devices with their start and end apart: 18, of which 11 were waited for; matrix products, arithmetic and copies ran while one was open for 0% of the time, Pallas kernels for 14%

profile of v1, /device:TPU:0, one launch (start us, length us, event | category | flops | bytes accessed | tf_op | source)
XLA Modules:
  0.0 122.0 jit_solution(16934317789669717766)
XLA Ops:
  2.2 3.0 %collective-permute-start = (f32[144,256]{1,0:T(8,128)S(1)}, f32[144,256]{1,0:T(8,128)S(1)}, u32[]{:S(2)}, u32[]{:S(2)}) collective-permute-start(f32[144,256]{1,0:T(8,128)S(1)} %get-tuple-element.29.refs_1_), channel_id=1, source_target_pairs={{0,2},{2,0},{1,3},{3,1},{4,6},{6,4},{5,7},{7,5},{8,10},{10,8},{9,1... | collective-permute-start | bytes 442376 | tf_op jit(solution)/shard_map/ppermute | solution.py:438
  5.3 3.8 %collective-permute-done.refs_2_ = f32[144,256]{1,0:T(8,128)S(1)} collective-permute-done((f32[144,256]{1,0:T(8,128)S(1)}, f32[144,256]{1,0:T(8,128)S(1)}, u32[]{:S(2)}, u32[]{:S(2)}) %collective-permute-start) | collective-permute-done | bytes 147488 | tf_op jit(solution)/shard_map/ppermute | solution.py:438
  9.1 1.9 %shard_map.93 = (f32[144,256]{1,0:T(8,128)S(1)}, f32[24,256]{1,0:T(8,128)S(1)}) custom-call(s32[5]{0:T(128)S(1)} %stack.22.refs_0_, f32[144,256]{1,0:T(8,128)S(1)} %get-tuple-element.29.refs_1_, f32[144,256]{1,0:T(8,128)S(1)} %collective-permute-done.refs_2_, f32[2,256,512]{2,1,0:T(8,128)S(1)} %copy-done.1, f32[2,512,256]{2,1,0:T(8,128)S(1)} %copy-done, ...), custom_call_target="tpu_custom_call" | custom-call | tf_op jit(solution)/shard_map/pallas_call | solution.py:439
  11.0 3.9 %collective-permute-start.4 = (f32[144,256]{1,0:T(8,128)S(1)}, f32[144,256]{1,0:T(8,128)S(1)}, u32[]{:S(2)}, u32[]{:S(2)}) collective-permute-start(f32[144,256]{1,0:T(8,128)S(1)} %get-tuple-element.34.refs_1_), channel_id=1, source_target_pairs={{0,12},{4,0},{8,4},{12,8},{1,13},{5,1},{9,5},{13,9},{2,14},{6,2},{... | collective-permute-start | bytes 442376 | tf_op jit(solution)/shard_map/ppermute | solution.py:451
  15.9 3.2 %collective-permute-done.4.refs_2_ = f32[144,256]{1,0:T(8,128)S(1)} collective-permute-done((f32[144,256]{1,0:T(8,128)S(1)}, f32[144,256]{1,0:T(8,128)S(1)}, u32[]{:S(2)}, u32[]{:S(2)}) %collective-permute-start.4) | collective-permute-done | bytes 147488 | tf_op jit(solution)/shard_map/ppermute | solution.py:451
  19.1 7.8 %collective-permute-done.3.refs_1_ = f32[144,256]{1,0:T(8,128)S(1)} collective-permute-done((f32[144,256]{1,0:T(8,128)S(1)}, f32[144,256]{1,0:T(8,128)S(1)}, u32[]{:S(2)}, u32[]{:S(2)}) %collective-permute-start.3) | collective-permute-done | bytes 147488 | tf_op jit(solution)/shard_map/ppermute | solution.py:451
  27.5 3.4 %load.9.refs_15_.refs_19_.refs_21_ = f32[16,512,256]{2,1,0:T(8,128)S(1)} custom-call(f32[64,512,256]{2,1,0:T(8,128)} %refs_22_.1, f32[144,256]{1,0:T(8,128)S(1)} %get-tuple-element.34.refs_1_), custom_call_target="tpu_custom_call" | custom-call | tf_op jit(solution)/shard_map/load/pallas_call | solution.py:98
  30.9 3.4 %load.8.refs_14_.refs_18_.refs_20_ = f32[16,512,256]{2,1,0:T(8,128)S(1)} custom-call(f32[64,512,256]{2,1,0:T(8,128)} %refs_0_.8, f32[144,256]{1,0:T(8,128)S(1)} %get-tuple-element.34.refs_1_), custom_call_target="tpu_custom_call" | custom-call | tf_op jit(solution)/shard_map/load/pallas_call | solution.py:98
  34.3 3.4 %load.7.refs_13_.refs_17_.refs_19_ = f32[16,512,256]{2,1,0:T(8,128)S(1)} custom-call(f32[64,512,256]{2,1,0:T(8,128)} %refs_0_.8, f32[144,256]{1,0:T(8,128)S(1)} %get-tuple-element.34.refs_1_), custom_call_target="tpu_custom_call" | custom-call | tf_op jit(solution)/shard_map/load/pallas_call | solution.py:98
  37.7 3.4 %load.6.refs_12_.refs_16_.refs_18_ = f32[16,512,256]{2,1,0:T(8,128)S(1)} custom-call(f32[64,512,256]{2,1,0:T(8,128)} %refs_0_.8, f32[144,256]{1,0:T(8,128)S(1)} %get-tuple-element.34.refs_1_), custom_call_target="tpu_custom_call" | custom-call | tf_op jit(solution)/shard_map/load/pallas_call | solution.py:98
  41.1 3.4 %load.5.refs_11_.refs_15_.refs_17_ = f32[16,512,256]{2,1,0:T(8,128)S(1)} custom-call(f32[64,512,256]{2,1,0:T(8,128)} %refs_0_.8, f32[144,256]{1,0:T(8,128)S(1)} %get-tuple-element.34.refs_1_), custom_call_target="tpu_custom_call" | custom-call | tf_op jit(solution)/shard_map/load/pallas_call | solution.py:98
  44.6 9.6 %shard_map.94 = (f32[64,256]{1,0:T(8,128)S(1)}, f32[64,256]{1,0:T(8,128)S(1)}, f32[5,8,256]{2,1,0:T(8,128)S(1)}, f32[5,8,256]{2,1,0:T(8,128)S(1)}, f32[144,256]{1,0:T(8,128)S(1)}) custom-call(s32[5]{0:T(128)S(1)} %stack.22.refs_0_, f32[144,256]{1,0:T(8,128)S(1)} %get-tuple-element.34.refs_1_, f32[144,256]{1,0:T(8,128)S(1)} %collective-permute-done.1.refs_2_, ...), custom_call_target="tpu_custom_call" | custom-call | tf_op jit(solution)/shard_map/pallas_call | solution.py:487
  54.2 1.6 %collective-permute-start.6 = (f32[144,256]{1,0:T(8,128)S(1)}, f32[144,256]{1,0:T(8,128)S(1)}, u32[]{:S(2)}, u32[]{:S(2)}) collective-permute-start(f32[144,256]{1,0:T(8,128)S(1)} %get-tuple-element.36.refs_1_), channel_id=1, source_target_pairs={{0,2},{2,0},{1,3},{3,1},{4,6},{6,4},{5,7},{7,5},{8,10},{10,8},{9,1... | collective-permute-start | bytes 442376 | tf_op jit(solution)/shard_map/ppermute | solution.py:438
  55.8 4.3 %collective-permute-done.6.refs_2_ = f32[144,256]{1,0:T(8,128)S(1)} collective-permute-done((f32[144,256]{1,0:T(8,128)S(1)}, f32[144,256]{1,0:T(8,128)S(1)}, u32[]{:S(2)}, u32[]{:S(2)}) %collective-permute-start.6) | collective-permute-done | bytes 147488 | tf_op jit(solution)/shard_map/ppermute | solution.py:438
  60.1 1.9 %shard_map.95 = (f32[136,256]{1,0:T(8,128)S(1)}, f32[24,256]{1,0:T(8,128)S(1)}) custom-call(s32[5]{0:T(128)S(1)} %stack.22.refs_0_, f32[144,256]{1,0:T(8,128)S(1)} %get-tuple-element.36.refs_1_, f32[144,256]{1,0:T(8,128)S(1)} %collective-permute-done.6.refs_2_, f32[2,256,512]{2,1,0:T(8,128)S(1)} %copy-done.1, f32[2,512,256]{2,1,0:T(8,128)S(1)} %copy-done, ...), custom_call_target="tpu_custom_call" | custom-call | tf_op jit(solution)/shard_map/pallas_call | solution.py:439
  64.5 1.9 %collective-permute-start.8 = (f32[136,256]{1,0:T(8,128)S(1)}, f32[136,256]{1,0:T(8,128)S(1)}, u32[]{:S(2)}, u32[]{:S(2)}) collective-permute-start(f32[136,256]{1,0:T(8,128)S(1)} %get-tuple-element.39.refs_1_), channel_id=1, source_target_pairs={{0,4},{4,8},{8,12},{12,0},{1,5},{5,9},{9,13},{13,1},{2,6},{6,10},{... | collective-permute-start | bytes 417800 | tf_op jit(solution)/shard_map/ppermute | solution.py:451
  67.8 8.6 %collective-permute-done.9.refs_1_ = f32[136,256]{1,0:T(8,128)S(1)} collective-permute-done((f32[136,256]{1,0:T(8,128)S(1)}, f32[136,256]{1,0:T(8,128)S(1)}, u32[]{:S(2)}, u32[]{:S(2)}) %collective-permute-start.9) | collective-permute-done | bytes 139296 | tf_op jit(solution)/shard_map/ppermute | solution.py:451
  78.5 9.6 %shard_map.96 = (f32[64,256]{1,0:T(8,128)S(1)}, f32[64,256]{1,0:T(8,128)S(1)}, f32[5,8,256]{2,1,0:T(8,128)S(1)}, f32[5,8,256]{2,1,0:T(8,128)S(1)}, f32[144,256]{1,0:T(8,128)S(1)}) custom-call(s32[5]{0:T(128)S(1)} %stack.22.refs_0_, f32[136,256]{1,0:T(8,128)S(1)} %get-tuple-element.39.refs_1_, f32[136,256]{1,0:T(8,128)S(1)} %collective-permute-done.7.refs_2_, ...), custom_call_target="tpu_custom_call" | custom-call | tf_op jit(solution)/shard_map/pallas_call | solution.py:487
  89.7 4.4 %collective-permute-done.12.refs_2_ = f32[144,256]{1,0:T(8,128)S(1)} collective-permute-done((f32[144,256]{1,0:T(8,128)S(1)}, f32[144,256]{1,0:T(8,128)S(1)}, u32[]{:S(2)}, u32[]{:S(2)}) %collective-permute-start.12) | collective-permute-done | bytes 147488 | tf_op jit(solution)/shard_map/ppermute | solution.py:438
  94.1 1.9 %shard_map.97 = (f32[136,256]{1,0:T(8,128)S(1)}, f32[24,256]{1,0:T(8,128)S(1)}) custom-call(s32[5]{0:T(128)S(1)} %stack.22.refs_0_, f32[144,256]{1,0:T(8,128)S(1)} %get-tuple-element.43.refs_1_, f32[144,256]{1,0:T(8,128)S(1)} %collective-permute-done.12.refs_2_, f32[2,256,512]{2,1,0:T(8,128)S(1)} %copy-done.1, f32[2,512,256]{2,1,0:T(8,128)S(1)} %copy-done, ...), custom_call_target="tpu_custom_call" | custom-call | tf_op jit(solution)/shard_map/pallas_call | solution.py:439
  97.4 1.9 %collective-permute-start.14 = (f32[136,256]{1,0:T(8,128)S(1)}, f32[136,256]{1,0:T(8,128)S(1)}, u32[]{:S(2)}, u32[]{:S(2)}) collective-permute-start(f32[136,256]{1,0:T(8,128)S(1)} %get-tuple-element.46.refs_1_), channel_id=1, source_target_pairs={{0,4},{4,8},{8,12},{12,0},{1,5},{5,9},{9,13},{13,1},{2,6},{6,10},{... | collective-permute-start | bytes 417800 | tf_op jit(solution)/shard_map/ppermute | solution.py:451
  99.3 2.5 %collective-permute-done.16.refs_2_ = f32[136,256]{1,0:T(8,128)S(1)} collective-permute-done((f32[136,256]{1,0:T(8,128)S(1)}, f32[136,256]{1,0:T(8,128)S(1)}, u32[]{:S(2)}, u32[]{:S(2)}) %collective-permute-start.16) | collective-permute-done | bytes 139296 | tf_op jit(solution)/shard_map/ppermute | solution.py:451
  101.9 7.5 %collective-permute-done.15.refs_1_ = f32[136,256]{1,0:T(8,128)S(1)} collective-permute-done((f32[136,256]{1,0:T(8,128)S(1)}, f32[136,256]{1,0:T(8,128)S(1)}, u32[]{:S(2)}, u32[]{:S(2)}) %collective-permute-start.15) | collective-permute-done | bytes 139296 | tf_op jit(solution)/shard_map/ppermute | solution.py:451
  111.4 10.4 %shard_map.98 = (f32[3,64,256]{2,1,0:T(8,128)}, f32[3,64,256]{2,1,0:T(8,128)}, f32[5,8,256]{2,1,0:T(8,128)}, f32[5,8,256]{2,1,0:T(8,128)}) custom-call(s32[5]{0:T(128)S(1)} %stack.22.refs_0_, f32[136,256]{1,0:T(8,128)S(1)} %get-tuple-element.46.refs_1_, f32[136,256]{1,0:T(8,128)S(1)} %collective-permute-done.13.refs_2_, f32[3,136,256]{2,1,0:T(8,128)S(1)} %stack.25.refs_3_, ...), custom_call_target="tpu_custom_call" | custom-call | tf_op jit(solution)/shard_map/pallas_call | solution.py:487
  (36 shorter events, 14.1 us)
Async XLA Ops:
  0.6 8.4 %copy-start = (f32[2,512,256]{2,1,0:T(8,128)S(1)}, f32[2,512,256]{2,1,0:T(8,128)}, u32[]{:S(2)}) copy-start(f32[2,512,256]{2,1,0:T(8,128)} %constant.24.clone.refs_4_) | copy-start | bytes 3145732
  0.6 8.4 %copy-start.1 = (f32[2,256,512]{2,1,0:T(8,128)S(1)}, f32[2,256,512]{2,1,0:T(8,128)}, u32[]{:S(2)}) copy-start(f32[2,256,512]{2,1,0:T(8,128)} %constant.23.clone.refs_3_) | copy-start | bytes 3145732
  0.7 8.4 %copy-start.3 = (f32[2,1,256]{2,1,0:T(1,128)S(1)}, f32[2,1,256]{2,1,0:T(1,128)}, u32[]{:S(2)}) copy-start(f32[2,1,256]{2,1,0:T(1,128)} %constant.25.clone.refs_5_) | copy-start | bytes 6148
  2.2 6.9 %collective-permute-start = (f32[144,256]{1,0:T(8,128)S(1)}, f32[144,256]{1,0:T(8,128)S(1)}, u32[]{:S(2)}, u32[]{:S(2)}) collective-permute-start(f32[144,256]{1,0:T(8,128)S(1)} %get-tuple-element.29.refs_1_), channel_id=1, source_target_pairs={{0,2},{2,0},{1,3},{3,1},{4,6},{6,4},{5,7},{7,5},{8,10},{10,8},{9,1... | collective-permute-start | bytes 442376 | tf_op jit(solution)/shard_map/ppermute | solution.py:438
  11.0 8.1 %collective-permute-start.4 = (f32[144,256]{1,0:T(8,128)S(1)}, f32[144,256]{1,0:T(8,128)S(1)}, u32[]{:S(2)}, u32[]{:S(2)}) collective-permute-start(f32[144,256]{1,0:T(8,128)S(1)} %get-tuple-element.34.refs_1_), channel_id=1, source_target_pairs={{0,12},{4,0},{8,4},{12,8},{1,13},{5,1},{9,5},{13,9},{2,14},{6,2},{... | collective-permute-start | bytes 442376 | tf_op jit(solution)/shard_map/ppermute | solution.py:451
  14.9 12.0 %collective-permute-start.3 = (f32[144,256]{1,0:T(8,128)S(1)}, f32[144,256]{1,0:T(8,128)S(1)}, u32[]{:S(2)}, u32[]{:S(2)}) collective-permute-start(f32[144,256]{1,0:T(8,128)S(1)} %get-tuple-element.34.refs_1_), channel_id=1, source_target_pairs={{0,8},{4,12},{8,0},{12,4},{1,9},{5,13},{9,1},{13,5},{2,10},{6,14},... | collective-permute-start | bytes 442376 | tf_op jit(solution)/shard_map/ppermute | solution.py:451
  14.9 12.0 %collective-permute-start.2 = (f32[144,256]{1,0:T(8,128)S(1)}, f32[144,256]{1,0:T(8,128)S(1)}, u32[]{:S(2)}, u32[]{:S(2)}) collective-permute-start(f32[144,256]{1,0:T(8,128)S(1)} %get-tuple-element.34.refs_1_), channel_id=1, source_target_pairs={{0,4},{4,8},{8,12},{12,0},{1,5},{5,9},{9,13},{13,1},{2,6},{6,10},{... | collective-permute-start | bytes 442376 | tf_op jit(solution)/shard_map/ppermute | solution.py:451
  26.9 17.6 %collective-permute-start.5 = (f32[3,144,256]{2,1,0:T(8,128)S(1)}, f32[3,144,256]{2,1,0:T(8,128)S(1)}, u32[]{:S(2)}, u32[]{:S(2)}) collective-permute-start(f32[3,144,256]{2,1,0:T(8,128)S(1)} %stack.23.refs_3_), channel_id=1, source_target_pairs={{0,1},{1,0},{2,3},{3,2},{4,5},{5,4},{6,7},{7,6},{8,9},{9,8},{10,11... | collective-permute-start | bytes 1327112 | tf_op jit(solution)/shard_map/ppermute | solution.py:466
  27.0 17.5 %collective-permute-start.1 = (f32[144,256]{1,0:T(8,128)S(1)}, f32[144,256]{1,0:T(8,128)S(1)}, u32[]{:S(2)}, u32[]{:S(2)}) collective-permute-start(f32[144,256]{1,0:T(8,128)S(1)} %get-tuple-element.34.refs_1_), channel_id=1, source_target_pairs={{0,1},{1,0},{2,3},{3,2},{4,5},{5,4},{6,7},{7,6},{8,9},{9,8},{10,11... | collective-permute-start | bytes 442376 | tf_op jit(solution)/shard_map/ppermute | solution.py:452
  41.1 3.4 %copy-start.2 = (f32[2,1,256]{2,1,0:T(1,128)S(1)}, f32[2,1,256]{2,1,0:T(1,128)}, u32[]{:S(2)}) copy-start(f32[2,1,256]{2,1,0:T(1,128)} %constant.26.clone.refs_6_) | copy-start | bytes 6148
  54.2 5.9 %collective-permute-start.6 = (f32[144,256]{1,0:T(8,128)S(1)}, f32[144,256]{1,0:T(8,128)S(1)}, u32[]{:S(2)}, u32[]{:S(2)}) collective-permute-start(f32[144,256]{1,0:T(8,128)S(1)} %get-tuple-element.36.refs_1_), channel_id=1, source_target_pairs={{0,2},{2,0},{1,3},{3,1},{4,6},{6,4},{5,7},{7,5},{8,10},{10,8},{9,1... | collective-permute-start | bytes 442376 | tf_op jit(solution)/shard_map/ppermute | solution.py:438
  62.0 5.8 %collective-permute-start.10 = (f32[136,256]{1,0:T(8,128)S(1)}, f32[136,256]{1,0:T(8,128)S(1)}, u32[]{:S(2)}, u32[]{:S(2)}) collective-permute-start(f32[136,256]{1,0:T(8,128)S(1)} %get-tuple-element.39.refs_1_), channel_id=1, source_target_pairs={{0,12},{4,0},{8,4},{12,8},{1,13},{5,1},{9,5},{13,9},{2,14},{6,2},{... | collective-permute-start | bytes 417800 | tf_op jit(solution)/shard_map/ppermute | solution.py:451
  63.0 13.4 %collective-permute-start.9 = (f32[136,256]{1,0:T(8,128)S(1)}, f32[136,256]{1,0:T(8,128)S(1)}, u32[]{:S(2)}, u32[]{:S(2)}) collective-permute-start(f32[136,256]{1,0:T(8,128)S(1)} %get-tuple-element.39.refs_1_), channel_id=1, source_target_pairs={{0,8},{4,12},{8,0},{12,4},{1,9},{5,13},{9,1},{13,5},{2,10},{6,14},... | collective-permute-start | bytes 417800 | tf_op jit(solution)/shard_map/ppermute | solution.py:451
  64.5 11.9 %collective-permute-start.8 = (f32[136,256]{1,0:T(8,128)S(1)}, f32[136,256]{1,0:T(8,128)S(1)}, u32[]{:S(2)}, u32[]{:S(2)}) collective-permute-start(f32[136,256]{1,0:T(8,128)S(1)} %get-tuple-element.39.refs_1_), channel_id=1, source_target_pairs={{0,4},{4,8},{8,12},{12,0},{1,5},{5,9},{9,13},{13,1},{2,6},{6,10},{... | collective-permute-start | bytes 417800 | tf_op jit(solution)/shard_map/ppermute | solution.py:451
  76.5 2.0 %collective-permute-start.11 = (f32[3,136,256]{2,1,0:T(8,128)S(1)}, f32[3,136,256]{2,1,0:T(8,128)S(1)}, u32[]{:S(2)}, u32[]{:S(2)}) collective-permute-start(f32[3,136,256]{2,1,0:T(8,128)S(1)} %stack.24.refs_3_), channel_id=1, source_target_pairs={{0,1},{1,0},{2,3},{3,2},{4,5},{5,4},{6,7},{7,6},{8,9},{9,8},{10,11... | collective-permute-start | bytes 1253384 | tf_op jit(solution)/shard_map/ppermute | solution.py:466
  76.5 1.9 %collective-permute-start.7 = (f32[136,256]{1,0:T(8,128)S(1)}, f32[136,256]{1,0:T(8,128)S(1)}, u32[]{:S(2)}, u32[]{:S(2)}) collective-permute-start(f32[136,256]{1,0:T(8,128)S(1)} %get-tuple-element.39.refs_1_), channel_id=1, source_target_pairs={{0,1},{1,0},{2,3},{3,2},{4,5},{5,4},{6,7},{7,6},{8,9},{9,8},{10,11... | collective-permute-start | bytes 417800 | tf_op jit(solution)/shard_map/ppermute | solution.py:452
  88.1 6.0 %collective-permute-start.12 = (f32[144,256]{1,0:T(8,128)S(1)}, f32[144,256]{1,0:T(8,128)S(1)}, u32[]{:S(2)}, u32[]{:S(2)}) collective-permute-start(f32[144,256]{1,0:T(8,128)S(1)} %get-tuple-element.43.refs_1_), channel_id=1, source_target_pairs={{0,2},{2,0},{1,3},{3,1},{4,6},{6,4},{5,7},{7,5},{8,10},{10,8},{9,1... | collective-permute-start | bytes 442376 | tf_op jit(solution)/shard_map/ppermute | solution.py:438
  96.0 5.8 %collective-permute-start.16 = (f32[136,256]{1,0:T(8,128)S(1)}, f32[136,256]{1,0:T(8,128)S(1)}, u32[]{:S(2)}, u32[]{:S(2)}) collective-permute-start(f32[136,256]{1,0:T(8,128)S(1)} %get-tuple-element.46.refs_1_), channel_id=1, source_target_pairs={{0,12},{4,0},{8,4},{12,8},{1,13},{5,1},{9,5},{13,9},{2,14},{6,2},{... | collective-permute-start | bytes 417800 | tf_op jit(solution)/shard_map/ppermute | solution.py:451
  96.1 13.3 %collective-permute-start.15 = (f32[136,256]{1,0:T(8,128)S(1)}, f32[136,256]{1,0:T(8,128)S(1)}, u32[]{:S(2)}, u32[]{:S(2)}) collective-permute-start(f32[136,256]{1,0:T(8,128)S(1)} %get-tuple-element.46.refs_1_), channel_id=1, source_target_pairs={{0,8},{4,12},{8,0},{12,4},{1,9},{5,13},{9,1},{13,5},{2,10},{6,14},... | collective-permute-start | bytes 417800 | tf_op jit(solution)/shard_map/ppermute | solution.py:451
  97.4 12.0 %collective-permute-start.14 = (f32[136,256]{1,0:T(8,128)S(1)}, f32[136,256]{1,0:T(8,128)S(1)}, u32[]{:S(2)}, u32[]{:S(2)}) collective-permute-start(f32[136,256]{1,0:T(8,128)S(1)} %get-tuple-element.46.refs_1_), channel_id=1, source_target_pairs={{0,4},{4,8},{8,12},{12,0},{1,5},{5,9},{9,13},{13,1},{2,6},{6,10},{... | collective-permute-start | bytes 417800 | tf_op jit(solution)/shard_map/ppermute | solution.py:451
  109.4 2.0 %collective-permute-start.17 = (f32[3,136,256]{2,1,0:T(8,128)S(1)}, f32[3,136,256]{2,1,0:T(8,128)S(1)}, u32[]{:S(2)}, u32[]{:S(2)}) collective-permute-start(f32[3,136,256]{2,1,0:T(8,128)S(1)} %stack.25.refs_3_), channel_id=1, source_target_pairs={{0,1},{1,0},{2,3},{3,2},{4,5},{5,4},{6,7},{7,6},{8,9},{9,8},{10,11... | collective-permute-start | bytes 1253384 | tf_op jit(solution)/shard_map/ppermute | solution.py:466
  109.5 1.9 %collective-permute-start.13 = (f32[136,256]{1,0:T(8,128)S(1)}, f32[136,256]{1,0:T(8,128)S(1)}, u32[]{:S(2)}, u32[]{:S(2)}) collective-permute-start(f32[136,256]{1,0:T(8,128)S(1)} %get-tuple-element.46.refs_1_), channel_id=1, source_target_pairs={{0,1},{1,0},{2,3},{3,2},{4,5},{5,4},{6,7},{7,6},{8,9},{9,8},{10,11... | collective-permute-start | bytes 417800 | tf_op jit(solution)/shard_map/ppermute | solution.py:452

commit v2 on v1

--- a/solution.py
+++ b/solution.py
@@ -17,7 +17,7 @@
 MASS_SQUARED = 1.0
 SUNSET_COUPLING = 100.0
 HARTREE_COUPLING = 2.45
-HIGHEST = lax.Precision.HIGHEST
+BF16 = np.dtype(jnp.bfloat16)
 
 SUB = 8
 LANES = 128
@@ -53,6 +53,21 @@
     backward = sine * (4.0 * math.pi * radius_step * radius[:, None]) / momentum[None, :]
     measure = momentum * momentum * momentum_step / (2.0 * math.pi**2)
     return tuple(np.asarray(a, np.float32) for a in (forward, backward, measure, momentum))
+
+
+def split(table):
+    high = table.astype(BF16)
+    return jnp.asarray(np.stack([high, (table - high.astype(np.float32)).astype(BF16)], axis=1))
+
+
+def product(value, table):
+    high = value.astype(jnp.bfloat16)
+    low = (value - high.astype(F32)).astype(jnp.bfloat16)
+
+    def dot(a, b):
+        return jnp.dot(a, b, preferred_element_type=F32)
+
+    return dot(high, table[0]) + (dot(high, table[1]) + dot(low, table[0]))
 
 
 def shifts(size, amount):
@@ -122,7 +137,7 @@
     tadpole = None
     for k in range(blocks):
         block = lax.rem(own + (blocks - k), blocks)
-        part = jnp.dot(pieces[k][...], forward[block], precision=HIGHEST, preferred_element_type=F32)
+        part = product(pieces[k][...], forward[block])
         radial = part if radial is None else radial + part
         line = rows - 1 if step == 0 else rows + current
         part = jnp.sum(pieces[k][line : line + 1, :] * measure[block], axis=1, keepdims=True)
@@ -134,7 +149,7 @@
     sigma_stat = -SUNSET_COUPLING * stat * (square_stat - 0.75 * square_spec)
     sigma_spec = -SUNSET_COUPLING * spec * (3.0 * square_stat - 0.25 * square_spec)
     sigma = jnp.concatenate([sigma_stat, sigma_spec], axis=0)
-    sigma = jnp.dot(sigma, backward[own], precision=HIGHEST, preferred_element_type=F32)
+    sigma = product(sigma, backward[own])
     group_stat = sigma[:rows]
     group_spec = sigma[half : half + rows]
     out_ref[0:rows, :] = group_stat
@@ -403,8 +418,8 @@
     half = rows + SUB
     hists, reps, moms = (lax.axis_size(a) for a in ("hist", "rep", "mom"))
     forward, backward, measure, momentum = tables(MOMENTA)
-    forward = jnp.asarray(forward.reshape(moms, width, MOMENTA))
-    backward = jnp.asarray(np.ascontiguousarray(backward.reshape(MOMENTA, moms, width).transpose(1, 0, 2)))
+    forward = split(forward.reshape(moms, width, MOMENTA))
+    backward = split(np.ascontiguousarray(backward.reshape(MOMENTA, moms, width).transpose(1, 0, 2)))
     measure = jnp.asarray(measure.reshape(moms, 1, width))
     own = lax.axis_index("mom")
     hist, rep = lax.axis_index("hist"), lax.axis_index("rep")
@@ -415,9 +430,9 @@
     keep = min(2 * rows, RESIDENT_BYTES // row_bytes // SUB * SUB)
     keep_stat = rows
     keep_spec = keep - rows
-    split = PART_ROWS
-    sizes_stat = [(r, min(split, keep_stat - r)) for r in range(0, keep_stat, split)]
-    sizes_spec = [(r, min(split, keep_spec - r)) for r in range(0, keep_spec, split)]
+    part = PART_ROWS
+    sizes_stat = [(r, min(part, keep_stat - r)) for r in range(0, keep_stat, part)]
+    sizes_spec = [(r, min(part, keep_spec - r)) for r in range(0, keep_spec, part)]
     stream = (keep_spec // SUB,) if keep_spec < rows else None
 
     c0, c1, d0, d1, send = pl.pallas_call(

time: 122 us -> 121 us (level)
  Pallas kernels: 53.9 us -> 52.4 us
    pallas_call x3, Pallas kernels: 5.7 us -> 4.18 us  [shards(): pl.pallas_call(functools.partial(transform_kernel, step, moms), in_specs=...]
where the time goes in v2:
time: 121 us; the launch traced here: 120 us
  Pallas kernels  52.4 us (43%)
  waiting for transfers between devices  46.5 us (38%)
  starting transfers between devices  20.5 us (17%)
    ppermute x9, waiting for transfers between devices, shards(): along.append(lax.ppermute(z, 'hist', shifts(hists, k)))  31.1 us
    pallas_call x3, Pallas kernels, shards(): pl.pallas_call(functools.partial(memory_kernel, step, (hists, reps), (siz...  29.7 us
    pallas_call x5, Pallas kernels, load(): pl.pallas_call(functools.partial(load_kernel, counts), out_shape=[pltpu.V...  17 us
    ppermute x9, starting transfers between devices, shards(): along.append(lax.ppermute(z, 'hist', shifts(hists, k)))  12.6 us
    ppermute x3, waiting for transfers between devices, shards(): pieces.append(lax.ppermute(send, 'mom', shifts(moms, k)))  12.5 us
    ppermute x3, starting transfers between devices, shards(): pieces.append(lax.ppermute(send, 'mom', shifts(moms, k)))  6.15 us
    pallas_call x3, Pallas kernels, shards(): pl.pallas_call(functools.partial(transform_kernel, step, moms), in_specs=...  4.18 us
    ppermute x3, waiting for transfers between devices, shards(): lax.ppermute(z, 'rep', shifts(reps, q))  2.9 us
  transfers between devices with their start and end apart: 18, of which 11 were waited for; matrix products, arithmetic and copies ran while one was open for 0% of the time, Pallas kernels for 14%

profile of v2, /device:TPU:0, one launch (start us, length us, event | category | flops | bytes accessed | tf_op | source)
XLA Modules:
  0.0 120.5 jit_solution(2951384578708623482)
XLA Ops:
  0.7 1.5 %first.1 = (f32[64,256]{1,0:T(8,128)S(1)}, f32[64,256]{1,0:T(8,128)S(1)}, f32[64,256]{1,0:T(8,128)S(1)}, f32[64,256]{1,0:T(8,128)S(1)}, f32[144,256]{1,0:T(8,128)S(1)}) custom-call(f32[64,512,256]{2,1,0:T(8,128)} %refs_0_.8, f32[64,512,256]{2,1,0:T(8,128)} %refs_22_.1), custom_call_target="tpu_custom_call" | custom-call | tf_op jit(solution)/shard_map/first/pallas_call | solution.py:438
  2.2 3.0 %collective-permute-start = (f32[144,256]{1,0:T(8,128)S(1)}, f32[144,256]{1,0:T(8,128)S(1)}, u32[]{:S(2)}, u32[]{:S(2)}) collective-permute-start(f32[144,256]{1,0:T(8,128)S(1)} %get-tuple-element.29.refs_1_), channel_id=1, source_target_pairs={{0,2},{2,0},{1,3},{3,1},{4,6},{6,4},{5,7},{7,5},{8,10},{10,8},{9,1... | collective-permute-start | bytes 442376 | tf_op jit(solution)/shard_map/ppermute | solution.py:453
  5.3 3.8 %collective-permute-done.refs_2_ = f32[144,256]{1,0:T(8,128)S(1)} collective-permute-done((f32[144,256]{1,0:T(8,128)S(1)}, f32[144,256]{1,0:T(8,128)S(1)}, u32[]{:S(2)}, u32[]{:S(2)}) %collective-permute-start) | collective-permute-done | bytes 147488 | tf_op jit(solution)/shard_map/ppermute | solution.py:453
  10.5 3.9 %collective-permute-start.4 = (f32[144,256]{1,0:T(8,128)S(1)}, f32[144,256]{1,0:T(8,128)S(1)}, u32[]{:S(2)}, u32[]{:S(2)}) collective-permute-start(f32[144,256]{1,0:T(8,128)S(1)} %get-tuple-element.34.refs_1_), channel_id=1, source_target_pairs={{0,12},{4,0},{8,4},{12,8},{1,13},{5,1},{9,5},{13,9},{2,14},{6,2},{... | collective-permute-start | bytes 442376 | tf_op jit(solution)/shard_map/ppermute | solution.py:466
  15.4 3.2 %collective-permute-done.4.refs_2_ = f32[144,256]{1,0:T(8,128)S(1)} collective-permute-done((f32[144,256]{1,0:T(8,128)S(1)}, f32[144,256]{1,0:T(8,128)S(1)}, u32[]{:S(2)}, u32[]{:S(2)}) %collective-permute-start.4) | collective-permute-done | bytes 147488 | tf_op jit(solution)/shard_map/ppermute | solution.py:466
  18.6 7.8 %collective-permute-done.3.refs_1_ = f32[144,256]{1,0:T(8,128)S(1)} collective-permute-done((f32[144,256]{1,0:T(8,128)S(1)}, f32[144,256]{1,0:T(8,128)S(1)}, u32[]{:S(2)}, u32[]{:S(2)}) %collective-permute-start.3) | collective-permute-done | bytes 147488 | tf_op jit(solution)/shard_map/ppermute | solution.py:466
  27.0 3.4 %load.9.refs_15_.refs_19_.refs_21_ = f32[16,512,256]{2,1,0:T(8,128)S(1)} custom-call(f32[64,512,256]{2,1,0:T(8,128)} %refs_22_.1, f32[144,256]{1,0:T(8,128)S(1)} %get-tuple-element.34.refs_1_), custom_call_target="tpu_custom_call" | custom-call | tf_op jit(solution)/shard_map/load/pallas_call | solution.py:113
  30.4 3.4 %load.8.refs_14_.refs_18_.refs_20_ = f32[16,512,256]{2,1,0:T(8,128)S(1)} custom-call(f32[64,512,256]{2,1,0:T(8,128)} %refs_0_.8, f32[144,256]{1,0:T(8,128)S(1)} %get-tuple-element.34.refs_1_), custom_call_target="tpu_custom_call" | custom-call | tf_op jit(solution)/shard_map/load/pallas_call | solution.py:113
  33.8 3.4 %load.7.refs_13_.refs_17_.refs_19_ = f32[16,512,256]{2,1,0:T(8,128)S(1)} custom-call(f32[64,512,256]{2,1,0:T(8,128)} %refs_0_.8, f32[144,256]{1,0:T(8,128)S(1)} %get-tuple-element.34.refs_1_), custom_call_target="tpu_custom_call" | custom-call | tf_op jit(solution)/shard_map/load/pallas_call | solution.py:113
  37.2 3.4 %load.6.refs_12_.refs_16_.refs_18_ = f32[16,512,256]{2,1,0:T(8,128)S(1)} custom-call(f32[64,512,256]{2,1,0:T(8,128)} %refs_0_.8, f32[144,256]{1,0:T(8,128)S(1)} %get-tuple-element.34.refs_1_), custom_call_target="tpu_custom_call" | custom-call | tf_op jit(solution)/shard_map/load/pallas_call | solution.py:113
  40.6 3.4 %load.5.refs_11_.refs_15_.refs_17_ = f32[16,512,256]{2,1,0:T(8,128)S(1)} custom-call(f32[64,512,256]{2,1,0:T(8,128)} %refs_0_.8, f32[144,256]{1,0:T(8,128)S(1)} %get-tuple-element.34.refs_1_), custom_call_target="tpu_custom_call" | custom-call | tf_op jit(solution)/shard_map/load/pallas_call | solution.py:113
  44.1 9.6 %shard_map.94 = (f32[64,256]{1,0:T(8,128)S(1)}, f32[64,256]{1,0:T(8,128)S(1)}, f32[5,8,256]{2,1,0:T(8,128)S(1)}, f32[5,8,256]{2,1,0:T(8,128)S(1)}, f32[144,256]{1,0:T(8,128)S(1)}) custom-call(s32[5]{0:T(128)S(1)} %stack.22.refs_0_, f32[144,256]{1,0:T(8,128)S(1)} %get-tuple-element.34.refs_1_, f32[144,256]{1,0:T(8,128)S(1)} %collective-permute-done.1.refs_2_, ...), custom_call_target="tpu_custom_call" | custom-call | tf_op jit(solution)/shard_map/pallas_call | solution.py:502
  53.7 1.6 %collective-permute-start.6 = (f32[144,256]{1,0:T(8,128)S(1)}, f32[144,256]{1,0:T(8,128)S(1)}, u32[]{:S(2)}, u32[]{:S(2)}) collective-permute-start(f32[144,256]{1,0:T(8,128)S(1)} %get-tuple-element.36.refs_1_), channel_id=1, source_target_pairs={{0,2},{2,0},{1,3},{3,1},{4,6},{6,4},{5,7},{7,5},{8,10},{10,8},{9,1... | collective-permute-start | bytes 442376 | tf_op jit(solution)/shard_map/ppermute | solution.py:453
  55.3 4.3 %collective-permute-done.6.refs_2_ = f32[144,256]{1,0:T(8,128)S(1)} collective-permute-done((f32[144,256]{1,0:T(8,128)S(1)}, f32[144,256]{1,0:T(8,128)S(1)}, u32[]{:S(2)}, u32[]{:S(2)}) %collective-permute-start.6) | collective-permute-done | bytes 147488 | tf_op jit(solution)/shard_map/ppermute | solution.py:453
  62.0 1.5 %collective-permute-start.9 = (f32[136,256]{1,0:T(8,128)S(1)}, f32[136,256]{1,0:T(8,128)S(1)}, u32[]{:S(2)}, u32[]{:S(2)}) collective-permute-start(f32[136,256]{1,0:T(8,128)S(1)} %get-tuple-element.39.refs_1_), channel_id=1, source_target_pairs={{0,8},{4,12},{8,0},{12,4},{1,9},{5,13},{9,1},{13,5},{2,10},{6,14},... | collective-permute-start | bytes 417800 | tf_op jit(solution)/shard_map/ppermute | solution.py:466
  63.5 1.9 %collective-permute-start.8 = (f32[136,256]{1,0:T(8,128)S(1)}, f32[136,256]{1,0:T(8,128)S(1)}, u32[]{:S(2)}, u32[]{:S(2)}) collective-permute-start(f32[136,256]{1,0:T(8,128)S(1)} %get-tuple-element.39.refs_1_), channel_id=1, source_target_pairs={{0,4},{4,8},{8,12},{12,0},{1,5},{5,9},{9,13},{13,1},{2,6},{6,10},{... | collective-permute-start | bytes 417800 | tf_op jit(solution)/shard_map/ppermute | solution.py:466
  66.8 8.6 %collective-permute-done.9.refs_1_ = f32[136,256]{1,0:T(8,128)S(1)} collective-permute-done((f32[136,256]{1,0:T(8,128)S(1)}, f32[136,256]{1,0:T(8,128)S(1)}, u32[]{:S(2)}, u32[]{:S(2)}) %collective-permute-start.9) | collective-permute-done | bytes 139296 | tf_op jit(solution)/shard_map/ppermute | solution.py:466
  77.5 9.6 %shard_map.96 = (f32[64,256]{1,0:T(8,128)S(1)}, f32[64,256]{1,0:T(8,128)S(1)}, f32[5,8,256]{2,1,0:T(8,128)S(1)}, f32[5,8,256]{2,1,0:T(8,128)S(1)}, f32[144,256]{1,0:T(8,128)S(1)}) custom-call(s32[5]{0:T(128)S(1)} %stack.22.refs_0_, f32[136,256]{1,0:T(8,128)S(1)} %get-tuple-element.39.refs_1_, f32[136,256]{1,0:T(8,128)S(1)} %collective-permute-done.7.refs_2_, ...), custom_call_target="tpu_custom_call" | custom-call | tf_op jit(solution)/shard_map/pallas_call | solution.py:502
  87.1 1.6 %collective-permute-start.12 = (f32[144,256]{1,0:T(8,128)S(1)}, f32[144,256]{1,0:T(8,128)S(1)}, u32[]{:S(2)}, u32[]{:S(2)}) collective-permute-start(f32[144,256]{1,0:T(8,128)S(1)} %get-tuple-element.43.refs_1_), channel_id=1, source_target_pairs={{0,2},{2,0},{1,3},{3,1},{4,6},{6,4},{5,7},{7,5},{8,10},{10,8},{9,1... | collective-permute-start | bytes 442376 | tf_op jit(solution)/shard_map/ppermute | solution.py:453
  88.7 4.4 %collective-permute-done.12.refs_2_ = f32[144,256]{1,0:T(8,128)S(1)} collective-permute-done((f32[144,256]{1,0:T(8,128)S(1)}, f32[144,256]{1,0:T(8,128)S(1)}, u32[]{:S(2)}, u32[]{:S(2)}) %collective-permute-start.12) | collective-permute-done | bytes 147488 | tf_op jit(solution)/shard_map/ppermute | solution.py:453
  95.9 1.9 %collective-permute-start.14 = (f32[136,256]{1,0:T(8,128)S(1)}, f32[136,256]{1,0:T(8,128)S(1)}, u32[]{:S(2)}, u32[]{:S(2)}) collective-permute-start(f32[136,256]{1,0:T(8,128)S(1)} %get-tuple-element.46.refs_1_), channel_id=1, source_target_pairs={{0,4},{4,8},{8,12},{12,0},{1,5},{5,9},{9,13},{13,1},{2,6},{6,10},{... | collective-permute-start | bytes 417800 | tf_op jit(solution)/shard_map/ppermute | solution.py:466
  97.8 2.5 %collective-permute-done.16.refs_2_ = f32[136,256]{1,0:T(8,128)S(1)} collective-permute-done((f32[136,256]{1,0:T(8,128)S(1)}, f32[136,256]{1,0:T(8,128)S(1)}, u32[]{:S(2)}, u32[]{:S(2)}) %collective-permute-start.16) | collective-permute-done | bytes 139296 | tf_op jit(solution)/shard_map/ppermute | solution.py:466
  100.3 7.5 %collective-permute-done.15.refs_1_ = f32[136,256]{1,0:T(8,128)S(1)} collective-permute-done((f32[136,256]{1,0:T(8,128)S(1)}, f32[136,256]{1,0:T(8,128)S(1)}, u32[]{:S(2)}, u32[]{:S(2)}) %collective-permute-start.15) | collective-permute-done | bytes 139296 | tf_op jit(solution)/shard_map/ppermute | solution.py:466
  109.9 10.4 %shard_map.98 = (f32[3,64,256]{2,1,0:T(8,128)}, f32[3,64,256]{2,1,0:T(8,128)}, f32[5,8,256]{2,1,0:T(8,128)}, f32[5,8,256]{2,1,0:T(8,128)}) custom-call(s32[5]{0:T(128)S(1)} %stack.22.refs_0_, f32[136,256]{1,0:T(8,128)S(1)} %get-tuple-element.46.refs_1_, f32[136,256]{1,0:T(8,128)S(1)} %collective-permute-done.13.refs_2_, f32[3,136,256]{2,1,0:T(8,128)S(1)} %stack.25.refs_3_, ...), custom_call_target="tpu_custom_call" | custom-call | tf_op jit(solution)/shard_map/pallas_call | solution.py:502
  (36 shorter events, 13.7 us)
Async XLA Ops:
  0.6 8.4 %copy-start = (bf16[2,2,512,256]{3,2,1,0:T(8,128)(2,1)S(1)}, bf16[2,2,512,256]{3,2,1,0:T(8,128)(2,1)}, u32[]{:S(2)}) copy-start(bf16[2,2,512,256]{3,2,1,0:T(8,128)(2,1)} %constant.24.clone.refs_4_) | copy-start | bytes 3145732
  0.6 8.4 %copy-start.1 = (bf16[2,2,256,512]{3,2,1,0:T(8,128)(2,1)S(1)}, bf16[2,2,256,512]{3,2,1,0:T(8,128)(2,1)}, u32[]{:S(2)}) copy-start(bf16[2,2,256,512]{3,2,1,0:T(8,128)(2,1)} %constant.23.clone.refs_3_) | copy-start | bytes 3145732
  0.7 8.4 %copy-start.3 = (f32[2,1,256]{2,1,0:T(1,128)S(1)}, f32[2,1,256]{2,1,0:T(1,128)}, u32[]{:S(2)}) copy-start(f32[2,1,256]{2,1,0:T(1,128)} %constant.25.clone.refs_5_) | copy-start | bytes 6148
  2.2 6.9 %collective-permute-start = (f32[144,256]{1,0:T(8,128)S(1)}, f32[144,256]{1,0:T(8,128)S(1)}, u32[]{:S(2)}, u32[]{:S(2)}) collective-permute-start(f32[144,256]{1,0:T(8,128)S(1)} %get-tuple-element.29.refs_1_), channel_id=1, source_target_pairs={{0,2},{2,0},{1,3},{3,1},{4,6},{6,4},{5,7},{7,5},{8,10},{10,8},{9,1... | collective-permute-start | bytes 442376 | tf_op jit(solution)/shard_map/ppermute | solution.py:453
  10.5 8.1 %collective-permute-start.4 = (f32[144,256]{1,0:T(8,128)S(1)}, f32[144,256]{1,0:T(8,128)S(1)}, u32[]{:S(2)}, u32[]{:S(2)}) collective-permute-start(f32[144,256]{1,0:T(8,128)S(1)} %get-tuple-element.34.refs_1_), channel_id=1, source_target_pairs={{0,12},{4,0},{8,4},{12,8},{1,13},{5,1},{9,5},{13,9},{2,14},{6,2},{... | collective-permute-start | bytes 442376 | tf_op jit(solution)/shard_map/ppermute | solution.py:466
  14.4 12.0 %collective-permute-start.3 = (f32[144,256]{1,0:T(8,128)S(1)}, f32[144,256]{1,0:T(8,128)S(1)}, u32[]{:S(2)}, u32[]{:S(2)}) collective-permute-start(f32[144,256]{1,0:T(8,128)S(1)} %get-tuple-element.34.refs_1_), channel_id=1, source_target_pairs={{0,8},{4,12},{8,0},{12,4},{1,9},{5,13},{9,1},{13,5},{2,10},{6,14},... | collective-permute-start | bytes 442376 | tf_op jit(solution)/shard_map/ppermute | solution.py:466
  14.4 12.0 %collective-permute-start.2 = (f32[144,256]{1,0:T(8,128)S(1)}, f32[144,256]{1,0:T(8,128)S(1)}, u32[]{:S(2)}, u32[]{:S(2)}) collective-permute-start(f32[144,256]{1,0:T(8,128)S(1)} %get-tuple-element.34.refs_1_), channel_id=1, source_target_pairs={{0,4},{4,8},{8,12},{12,0},{1,5},{5,9},{9,13},{13,1},{2,6},{6,10},{... | collective-permute-start | bytes 442376 | tf_op jit(solution)/shard_map/ppermute | solution.py:466
  26.4 17.6 %collective-permute-start.5 = (f32[3,144,256]{2,1,0:T(8,128)S(1)}, f32[3,144,256]{2,1,0:T(8,128)S(1)}, u32[]{:S(2)}, u32[]{:S(2)}) collective-permute-start(f32[3,144,256]{2,1,0:T(8,128)S(1)} %stack.23.refs_3_), channel_id=1, source_target_pairs={{0,1},{1,0},{2,3},{3,2},{4,5},{5,4},{6,7},{7,6},{8,9},{9,8},{10,11... | collective-permute-start | bytes 1327112 | tf_op jit(solution)/shard_map/ppermute | solution.py:481
  26.5 17.5 %collective-permute-start.1 = (f32[144,256]{1,0:T(8,128)S(1)}, f32[144,256]{1,0:T(8,128)S(1)}, u32[]{:S(2)}, u32[]{:S(2)}) collective-permute-start(f32[144,256]{1,0:T(8,128)S(1)} %get-tuple-element.34.refs_1_), channel_id=1, source_target_pairs={{0,1},{1,0},{2,3},{3,2},{4,5},{5,4},{6,7},{7,6},{8,9},{9,8},{10,11... | collective-permute-start | bytes 442376 | tf_op jit(solution)/shard_map/ppermute | solution.py:467
  40.6 3.4 %copy-start.2 = (f32[2,1,256]{2,1,0:T(1,128)S(1)}, f32[2,1,256]{2,1,0:T(1,128)}, u32[]{:S(2)}) copy-start(f32[2,1,256]{2,1,0:T(1,128)} %constant.26.clone.refs_6_) | copy-start | bytes 6148
  53.7 5.9 %collective-permute-start.6 = (f32[144,256]{1,0:T(8,128)S(1)}, f32[144,256]{1,0:T(8,128)S(1)}, u32[]{:S(2)}, u32[]{:S(2)}) collective-permute-start(f32[144,256]{1,0:T(8,128)S(1)} %get-tuple-element.36.refs_1_), channel_id=1, source_target_pairs={{0,2},{2,0},{1,3},{3,1},{4,6},{6,4},{5,7},{7,5},{8,10},{10,8},{9,1... | collective-permute-start | bytes 442376 | tf_op jit(solution)/shard_map/ppermute | solution.py:453
  61.0 5.8 %collective-permute-start.10 = (f32[136,256]{1,0:T(8,128)S(1)}, f32[136,256]{1,0:T(8,128)S(1)}, u32[]{:S(2)}, u32[]{:S(2)}) collective-permute-start(f32[136,256]{1,0:T(8,128)S(1)} %get-tuple-element.39.refs_1_), channel_id=1, source_target_pairs={{0,12},{4,0},{8,4},{12,8},{1,13},{5,1},{9,5},{13,9},{2,14},{6,2},{... | collective-permute-start | bytes 417800 | tf_op jit(solution)/shard_map/ppermute | solution.py:466
  62.0 13.4 %collective-permute-start.9 = (f32[136,256]{1,0:T(8,128)S(1)}, f32[136,256]{1,0:T(8,128)S(1)}, u32[]{:S(2)}, u32[]{:S(2)}) collective-permute-start(f32[136,256]{1,0:T(8,128)S(1)} %get-tuple-element.39.refs_1_), channel_id=1, source_target_pairs={{0,8},{4,12},{8,0},{12,4},{1,9},{5,13},{9,1},{13,5},{2,10},{6,14},... | collective-permute-start | bytes 417800 | tf_op jit(solution)/shard_map/ppermute | solution.py:466
  63.5 11.9 %collective-permute-start.8 = (f32[136,256]{1,0:T(8,128)S(1)}, f32[136,256]{1,0:T(8,128)S(1)}, u32[]{:S(2)}, u32[]{:S(2)}) collective-permute-start(f32[136,256]{1,0:T(8,128)S(1)} %get-tuple-element.39.refs_1_), channel_id=1, source_target_pairs={{0,4},{4,8},{8,12},{12,0},{1,5},{5,9},{9,13},{13,1},{2,6},{6,10},{... | collective-permute-start | bytes 417800 | tf_op jit(solution)/shard_map/ppermute | solution.py:466
  75.5 2.0 %collective-permute-start.11 = (f32[3,136,256]{2,1,0:T(8,128)S(1)}, f32[3,136,256]{2,1,0:T(8,128)S(1)}, u32[]{:S(2)}, u32[]{:S(2)}) collective-permute-start(f32[3,136,256]{2,1,0:T(8,128)S(1)} %stack.24.refs_3_), channel_id=1, source_target_pairs={{0,1},{1,0},{2,3},{3,2},{4,5},{5,4},{6,7},{7,6},{8,9},{9,8},{10,11... | collective-permute-start | bytes 1253384 | tf_op jit(solution)/shard_map/ppermute | solution.py:481
  75.5 1.9 %collective-permute-start.7 = (f32[136,256]{1,0:T(8,128)S(1)}, f32[136,256]{1,0:T(8,128)S(1)}, u32[]{:S(2)}, u32[]{:S(2)}) collective-permute-start(f32[136,256]{1,0:T(8,128)S(1)} %get-tuple-element.39.refs_1_), channel_id=1, source_target_pairs={{0,1},{1,0},{2,3},{3,2},{4,5},{5,4},{6,7},{7,6},{8,9},{9,8},{10,11... | collective-permute-start | bytes 417800 | tf_op jit(solution)/shard_map/ppermute | solution.py:467
  87.1 6.0 %collective-permute-start.12 = (f32[144,256]{1,0:T(8,128)S(1)}, f32[144,256]{1,0:T(8,128)S(1)}, u32[]{:S(2)}, u32[]{:S(2)}) collective-permute-start(f32[144,256]{1,0:T(8,128)S(1)} %get-tuple-element.43.refs_1_), channel_id=1, source_target_pairs={{0,2},{2,0},{1,3},{3,1},{4,6},{6,4},{5,7},{7,5},{8,10},{10,8},{9,1... | collective-permute-start | bytes 442376 | tf_op jit(solution)/shard_map/ppermute | solution.py:453
  94.5 5.9 %collective-permute-start.16 = (f32[136,256]{1,0:T(8,128)S(1)}, f32[136,256]{1,0:T(8,128)S(1)}, u32[]{:S(2)}, u32[]{:S(2)}) collective-permute-start(f32[136,256]{1,0:T(8,128)S(1)} %get-tuple-element.46.refs_1_), channel_id=1, source_target_pairs={{0,12},{4,0},{8,4},{12,8},{1,13},{5,1},{9,5},{13,9},{2,14},{6,2},{... | collective-permute-start | bytes 417800 | tf_op jit(solution)/shard_map/ppermute | solution.py:466
  94.6 13.3 %collective-permute-start.15 = (f32[136,256]{1,0:T(8,128)S(1)}, f32[136,256]{1,0:T(8,128)S(1)}, u32[]{:S(2)}, u32[]{:S(2)}) collective-permute-start(f32[136,256]{1,0:T(8,128)S(1)} %get-tuple-element.46.refs_1_), channel_id=1, source_target_pairs={{0,8},{4,12},{8,0},{12,4},{1,9},{5,13},{9,1},{13,5},{2,10},{6,14},... | collective-permute-start | bytes 417800 | tf_op jit(solution)/shard_map/ppermute | solution.py:466
  95.9 12.0 %collective-permute-start.14 = (f32[136,256]{1,0:T(8,128)S(1)}, f32[136,256]{1,0:T(8,128)S(1)}, u32[]{:S(2)}, u32[]{:S(2)}) collective-permute-start(f32[136,256]{1,0:T(8,128)S(1)} %get-tuple-element.46.refs_1_), channel_id=1, source_target_pairs={{0,4},{4,8},{8,12},{12,0},{1,5},{5,9},{9,13},{13,1},{2,6},{6,10},{... | collective-permute-start | bytes 417800 | tf_op jit(solution)/shard_map/ppermute | solution.py:466
  107.9 2.0 %collective-permute-start.17 = (f32[3,136,256]{2,1,0:T(8,128)S(1)}, f32[3,136,256]{2,1,0:T(8,128)S(1)}, u32[]{:S(2)}, u32[]{:S(2)}) collective-permute-start(f32[3,136,256]{2,1,0:T(8,128)S(1)} %stack.25.refs_3_), channel_id=1, source_target_pairs={{0,1},{1,0},{2,3},{3,2},{4,5},{5,4},{6,7},{7,6},{8,9},{9,8},{10,11... | collective-permute-start | bytes 1253384 | tf_op jit(solution)/shard_map/ppermute | solution.py:481
  108.0 1.9 %collective-permute-start.13 = (f32[136,256]{1,0:T(8,128)S(1)}, f32[136,256]{1,0:T(8,128)S(1)}, u32[]{:S(2)}, u32[]{:S(2)}) collective-permute-start(f32[136,256]{1,0:T(8,128)S(1)} %get-tuple-element.46.refs_1_), channel_id=1, source_target_pairs={{0,1},{1,0},{2,3},{3,2},{4,5},{5,4},{6,7},{7,6},{8,9},{9,8},{10,11... | collective-permute-start | bytes 417800 | tf_op jit(solution)/shard_map/ppermute | solution.py:467
